TPU v7x, 512 devices: a whole 4x8x8 slice. The times are simulated.
512 devices in a mesh: gy: 32 (over z, y_lo), gz: 16 (over x, y_hi, core).
Axes of the slice: x: 4, y: 8 (y_hi: 2, y_lo: 4; y = y_hi * 4 + y_lo), z: 8, core: 2. Of those that a mesh axis runs over, the one named last changes fastest.
Arguments:
- scalar: float32 [64, 768, 768], P('gz', 'gy'), may hold values from -6 to 6
- velocity: float32 [3, 64, 256, 256], P(None, None, 'gy', 'gz'), may hold values from -0.9 to 0.9
Outputs:
- remeshed: float32 [64, 768, 768], P('gz', 'gy')
All inputs are finite; a program needn't handle non-finite values.
Results may differ from a plain program's by a relative error of at most 0.0003.
Values sent between devices are 32-bit elements; how exact they have to be, the bound alone decides.
A program may use at most 64 MiB of HBM per device.

v0:
```python
import functools

import jax
import jax.numpy as jnp
import numpy as np
from jax import lax
from jax.experimental import pallas as pl
from jax.experimental.pallas import tpu as pltpu
from jax.sharding import PartitionSpec as P

LANES = 128
INNER = [1.0, 0.0, -5.0 / 4.0, -35.0 / 12.0, 21.0 / 4.0, -25.0 / 12.0]
MIDDLE = [-4.0, 75.0 / 4.0, -245.0 / 8.0, 545.0 / 24.0, -63.0 / 8.0, 25.0 / 24.0]
OUTER = [18.0, -153.0 / 4.0, 255.0 / 8.0, -313.0 / 24.0, 21.0 / 8.0, -5.0 / 24.0]


def shifted(factors, base, slope):
    total = np.polynomial.Polynomial([0.0])
    for factor in reversed(factors):
        total = total * np.polynomial.Polynomial([base, slope]) + factor
    coefs = np.zeros(6)
    coefs[: len(total.coef)] = total.coef
    return [0.0 if abs(c) < 1e-10 else float(c) for c in coefs]


AHEAD = {1: shifted(INNER, 1.0, -1.0), 2: shifted(MIDDLE, 2.0, -1.0), 3: shifted(OUTER, 3.0, -1.0)}
BEHIND = {1: shifted(MIDDLE, 1.0, 1.0), 2: shifted(OUTER, 2.0, 1.0)}


def horner(factors, value):
    lowest = 0
    while factors[lowest] == 0.0:
        lowest += 1
    result = jnp.full_like(value, factors[-1])
    for factor in reversed(factors[lowest:-1]):
        result = result * value
        if factor != 0.0:
            result = result + factor
    for _ in range(lowest):
        result = result * value
    return result


def weights(moved):
    size = jnp.abs(moved)
    positive = moved >= 0.0
    result = {0: horner(INNER, size)}
    for m in (1, 2, 3):
        near = horner(AHEAD[m], size)
        far = horner(BEHIND[m], size) if m in BEHIND else jnp.zeros_like(size)
        result[m] = jnp.where(positive, near, far)
        result[-m] = jnp.where(positive, far, near)
    return result


def displacement(speed, before, after):
    return speed + 0.5 * speed * jnp.where(speed >= 0.0, after - speed, speed - before)


def roll(value, shift, axis):
    return pltpu.roll(value, shift % value.shape[axis], axis)


def sweep_periodic(field, speed, axis):
    moved = displacement(speed, roll(speed, 1, axis), roll(speed, -1, axis))
    w = weights(moved)
    result = field * w[0]
    for m in (-3, -2, -1, 1, 2, 3):
        result = result + roll(field * w[m], m, axis)
    return result


def dot(a, b, dims=((1,), (0,))):
    return lax.dot_general(
        a, b, (dims, ((), ())), precision=lax.Precision.HIGHEST, preferred_element_type=jnp.float32
    )


def refine(coarse):
    out = np.zeros((coarse, 3 * coarse), np.float32)
    for c in range(coarse):
        for k in range(3):
            out[c, 3 * c + k] += 1.0 - k / 3.0
            out[(c + 1) % coarse, 3 * c + k] += k / 3.0
    return out


def refine_block(count):
    out = np.zeros((2 * count, 3 * count), np.float32)
    for c in range(count):
        for k in range(3):
            out[c, 3 * c + k] += 1.0 - k / 3.0
            out[c + 1, 3 * c + k] += k / 3.0
    return out


def constants(nz, gz, gy, yc, xc):
    bc = gz * xc // gy
    full = refine(gz * xc)
    ex = full.reshape(gz, xc, -1)
    block = refine_block(yc)
    rows = np.zeros((nz * 3 * yc, 2 * nz * yc), np.float32)
    for z in range(nz):
        for part in range(2):
            at = part * nz * yc + z * yc
            rows[z * 3 * yc : (z + 1) * 3 * yc, at : at + yc] = block[part * yc : (part + 1) * yc].T
    block = refine_block(bc)
    planes = 2 * nz + 2
    xy = np.zeros((2 * LANES, LANES), np.float32)
    xz = np.zeros(((nz + 2) * 3 * bc, 2 * LANES), np.float32)
    for plane in range(planes):
        for part in range(2):
            at = part * LANES + plane * (bc + 1)
            piece = block[bc : bc + 1] if part else block[: bc + 1]
            end = at + len(piece)
            if plane < nz:
                xy[at:end, plane * 3 * bc : (plane + 1) * 3 * bc] = piece
            else:
                z = plane - nz
                xz[z * 3 * bc : (z + 1) * 3 * bc, at:end] = piece.T
    ey = refine(gy * yc)
    return rows, ex, xy, xz, ey, np.ascontiguousarray(ey.T)


def wrapped(index, size):
    return jnp.where(index >= size, index - size, index)


def kernel(gz, gy, nz, yc, xc, *refs):
    (scalar_hbm, vel_hbm, rows_hbm, ex_hbm, xy_hbm, xz_hbm, ey_hbm, eyt_hbm, out,
     scalar, vel, rows_m, ex_m, xy_m, xz_m, ey_m, eyt_m,
     own, nxt, vsend, v0, v1, blocks, pencil, up_out, down_out, up_in, down_in,
     local_sem, own_s, own_r, nxt_s, nxt_r, v0_s, v0_r, v1_s, v1_r, blk_s, blk_r, z_s, z_r) = refs
    h = lax.axis_index("gz")
    s = lax.axis_index("gy")
    rf = 3 * yc
    bc = gz * xc // gy
    bf = 3 * bc
    per = gy // gz
    behind = wrapped(s + gy - 1, gy)
    at_end = lax.rem(s, per) == per - 1
    total = gz * nz

    loads = []
    for i, (src, dst) in enumerate((
        (vel_hbm, vel), (scalar_hbm, scalar), (rows_hbm, rows_m), (ex_hbm, ex_m), (xy_hbm, xy_m),
        (xz_hbm, xz_m), (ey_hbm, ey_m), (eyt_hbm, eyt_m),
    )):
        load = pltpu.make_async_copy(src, dst, local_sem.at[i])
        load.start()
        loads.append(load)

    barrier = pltpu.get_barrier_semaphore()
    everyone = gz * gy

    def greet(step, p):
        pl.semaphore_signal(
            barrier, inc=1, device_id={"gz": p, "gy": wrapped(s + step, gy)},
            device_id_type=pl.DeviceIdType.MESH,
        )

    def greet_all(step, _):
        for i in range(gz):
            greet(step, wrapped(h + i, gz))
        return 0

    for i in range(1, gz):
        greet(0, wrapped(h + i, gz))
    lax.fori_loop(1, gy, greet_all, 0, unroll=gz * gy <= 64)

    def remote(src, dst, send, recv, p, g):
        return pltpu.make_async_remote_copy(
            src_ref=src, dst_ref=dst, send_sem=send, recv_sem=recv,
            device_id={"gz": p, "gy": g}, device_id_type=pl.DeviceIdType.MESH,
        )

    def ux_copies(step):
        p = wrapped(h + step, gz)
        planes = vel.at[0, pl.ds(p * nz, nz)]
        first = (
            pltpu.make_async_copy(planes, own.at[h], own_r.at[h])
            if step == 0
            else remote(planes, own.at[h], own_s.at[step], own_r.at[h], p, s)
        )
        return first, remote(planes, nxt.at[h], nxt_s.at[step], nxt_r.at[h], p, behind)

    loads[0].wait()
    lane = lax.broadcasted_iota(jnp.int32, (yc, LANES), 1)
    fill = jnp.zeros((yc, LANES - xc), jnp.float32)
    def wide_plane(value):
        return jnp.concatenate([value, fill], axis=1)

    for p in range(gz):
        planes = [wide_plane(vel[1, p * nz + z]) for z in range(nz)]
        for z in range(p * nz - 1, p * nz + nz + 1):
            planes.append(wide_plane(vel[2, z]) if 0 <= z < total else None)
        for c in range(per):
            tile = jnp.zeros((yc, LANES), jnp.float32)
            for i, plane in enumerate(planes):
                if plane is not None:
                    tile = jnp.where(
                        (lane >= i * (bc + 1)) & (lane < i * (bc + 1) + min(bc + 1, xc - c * bc)),
                        roll(plane, i * (bc + 1) - c * bc, 1),
                        tile,
                    )
            vsend[p, c] = tile


    @pl.when(jnp.logical_not(at_end))
    def _():
        v1[...] = jnp.zeros(v1.shape, jnp.float32)

    pl.semaphore_wait(barrier, everyone - 1)
    ux = [ux_copies(step) for step in range(gz)]
    for first, second in ux:
        second.start()
        first.start()

    def v_copies(p, c, first, act, own_too):
        if first:
            dst_buf, send, recv, g = v0, v0_s.at[p * per + c], v0_r, h * per + c
        else:
            dst_buf, send, recv, g = v1, v1_s.at[p], v1_r, wrapped(h * per + c + gy - 1, gy)
        mine = (p == h) & (g == s)

        @pl.when(jnp.logical_not(mine))
        def _():
            act(remote(vsend.at[p, c], dst_buf.at[s], send, recv.at[s], p, g))

        if own_too:
            @pl.when(mine)
            def _():
                act(pltpu.make_async_copy(vsend.at[p, c], dst_buf.at[s], recv.at[s]))

    v_tiles = [(p, c, first) for p in range(gz) for first in (True, False)
               for c in (range(per) if first else range(1))]
    for p, c, first in v_tiles:
        v_copies(p, c, first, lambda copy: copy.start(), True)

    for load in loads[1:4]:
        load.wait()
    count = nz * yc
    speed = None
    for i in range(gz):
        pltpu.make_async_copy(own.at[i], own.at[i], own_r.at[i]).wait()
        pltpu.make_async_copy(nxt.at[i], nxt.at[i], nxt_r.at[i]).wait()
        coarse = jnp.concatenate(
            [own[i].reshape(count, xc), nxt[i].reshape(count, xc)], axis=0
        )
        part = dot(dot(rows_m[...], coarse), ex_m[i])
        speed = part if speed is None else speed + part
    nx = scalar.shape[2]
    field = scalar[...].reshape(nz * rf, nx)
    field = sweep_periodic(field, speed, 1)

    wide = lax.broadcasted_iota(jnp.int32, (rf, LANES), 1)
    for g in range(gy):
        low = g * bf
        first, last = low // LANES, (low + bf - 1) // LANES
        tile = jnp.zeros((rf, LANES), jnp.float32)
        for z in range(nz):
            for t in range(first, last + 1):
                piece = field[z * rf : (z + 1) * rf, t * LANES : (t + 1) * LANES]
                begin = z * bf + max(0, t * LANES - low)
                end = z * bf + min(bf, (t + 1) * LANES - low)
                tile = jnp.where(
                    (wide >= begin) & (wide < end), roll(piece, z * bf - low, 1), tile
                )
        blocks[g] = tile

    def block_copy(step):
        g = wrapped(s + step, gy)
        if step == 0:
            return pltpu.make_async_copy(blocks.at[g], pencil.at[s], blk_r.at[s])
        return remote(blocks.at[g], pencil.at[s], blk_s.at[step], blk_r.at[s], h, g)

    sends = [block_copy(step) for step in range(gy)]
    for copy in sends[1:] + sends[:1]:
        copy.start()

    for load in loads[4:]:
        load.wait()
    for i in range(gy):
        pltpu.make_async_copy(v0.at[i], v0.at[i], v0_r.at[i]).wait()

    @pl.when(at_end)
    def _():
        for i in range(gy):
            pltpu.make_async_copy(v1.at[i], v1.at[i], v1_r.at[i]).wait()

    nyc = gy * yc
    coarse = jnp.concatenate(
        [v0[...].reshape(nyc, LANES), v1[...].reshape(nyc, LANES)], axis=1
    )
    speed_y = dot(eyt_m[...], dot(coarse, xy_m[...]))
    speed_z = dot(dot(xz_m[...], coarse, ((1,), (1,))), ey_m[...])

    for i in range(gy):
        pltpu.make_async_copy(pencil.at[i], pencil.at[i], blk_r.at[i]).wait()
    field = pencil[...].reshape(gy * rf, LANES)
    field = sweep_periodic(field, speed_y, 0)

    ny = gy * rf
    chunks = ny // LANES
    below, above = wrapped(h + gz - 1, gz), wrapped(h + 1, gz)
    ups, downs = [], []
    for k in range(chunks):
        cols = slice(k * LANES, (k + 1) * LANES)
        part = jnp.transpose(field[cols])[: nz * bf]
        moved = displacement(
            speed_z[bf : (nz + 1) * bf, cols], speed_z[: nz * bf, cols], speed_z[2 * bf :, cols]
        )
        w = weights(moved)

        def landing(target):
            result = None
            for m in range(-3, 4):
                z = target - m
                if 0 <= z < nz:
                    at = slice(z * bf, (z + 1) * bf)
                    term = part[at] * w[m][at]
                    result = term if result is None else result + term
            return result

        for i in range(3):
            up_out[k, i] = landing(nz + i)
            down_out[k, i] = landing(i - 3)
        up = remote(up_out.at[k], up_in.at[k], z_s.at[0, k], z_r.at[0, k], above, s)
        down = remote(down_out.at[k], down_in.at[k], z_s.at[1, k], z_r.at[1, k], below, s)
        ups.append(up)
        downs.append(down)

        @pl.when(h < gz - 1)
        def _():
            up.start()

        @pl.when(h > 0)
        def _():
            down.start()

        for i in range(nz):
            out[i, :, cols] = landing(i)

    @pl.when(h > 0)
    def _():
        for k in range(chunks):
            cols = slice(k * LANES, (k + 1) * LANES)
            ups[k].wait_recv()
            for i in range(3):
                out[i, :, cols] = out[i, :, cols] + up_in[k, i]
        for copy in downs:
            copy.wait_send()

    @pl.when(h < gz - 1)
    def _():
        for k in range(chunks):
            cols = slice(k * LANES, (k + 1) * LANES)
            downs[k].wait_recv()
            for i in range(nz - 3, nz):
                out[i, :, cols] = out[i, :, cols] + down_in[k, i - nz + 3]
        for copy in ups:
            copy.wait_send()

    for step, (first, second) in enumerate(ux):
        if step:
            first.wait_send()
        second.wait_send()
    for copy in sends[1:]:
        copy.wait_send()
    for p, c, first in v_tiles:
        v_copies(p, c, first, lambda copy: copy.wait_send(), False)


def local(scalar, velocity):
    gz, gy = lax.axis_size("gz"), lax.axis_size("gy")
    nz, rf, nx = scalar.shape
    yc, xc = velocity.shape[2:]
    bc = gz * xc // gy
    bf = 3 * bc
    ny = gy * rf
    mats = constants(nz, gz, gy, yc, xc)
    per = gy // gz
    f32 = jnp.float32
    dma = pltpu.SemaphoreType.DMA
    anywhere = pl.BlockSpec(memory_space=pl.ANY)
    vmem = pl.BlockSpec(memory_space=pltpu.VMEM)
    scratch = [pltpu.VMEM(scalar.shape, f32), pltpu.VMEM(velocity.shape, f32)]
    scratch += [pltpu.VMEM(m.shape, f32) for m in mats]
    scratch += [
        pltpu.VMEM((gz, nz, yc, xc), f32),
        pltpu.VMEM((gz, nz, yc, xc), f32),
        pltpu.VMEM((gz, per, yc, LANES), f32),
        pltpu.VMEM((gy, yc, LANES), f32),
        pltpu.VMEM((gy, yc, LANES), f32),
        pltpu.VMEM((gy, rf, LANES), f32),
        pltpu.VMEM((gy, rf, LANES), f32),
    ]
    scratch += [pltpu.VMEM((ny // LANES, 3, bf, LANES), f32)] * 4
    scratch += [dma((n,)) for n in (
        2 + len(mats), gz, gz, gz, gz, gz * per, gy, gz, gy, gy, gy
    )]
    scratch += [dma((2, ny // LANES))] * 2
    return pl.pallas_call(
        functools.partial(kernel, gz, gy, nz, yc, xc),
        out_shape=pltpu.VMEM((nz, bf, ny), f32),
        in_specs=[anywhere] * (2 + len(mats)),
        out_specs=vmem,
        scratch_shapes=scratch,
        compiler_params=pltpu.CompilerParams(has_side_effects=True, collective_id=0),
    )(scalar, velocity, *[jnp.asarray(m) for m in mats])


def solution(mesh):
    in_specs = (P("gz", "gy", None), P(None, None, "gy", "gz"))
    out_specs = P("gz", "gy", None)
    return jax.shard_map(local, mesh=mesh, in_specs=in_specs, out_specs=out_specs, check_vma=False)
```

profile of v0, /device:TPU:1, one launch (start us, length us, event | category | flops | bytes accessed | tf_op | source)
XLA Modules:
  0.0 75.3 jit_solution(16893551753584533872)
XLA Ops:
  0.0 2.1 %copy.9.refs_1_ = f32[3,64,8,16]{3,2,1,0:T(8,128)} copy(f32[3,64,8,16]{1,3,2,0:T(8,128)} %param.9) | data formatting | bytes 196608 | tf_op args[1]
  2.1 72.5 %shard_map.82 = f32[4,24,768]{2,1,0:T(8,128)S(1)} custom-call(f32[4,24,768]{2,1,0:T(8,128)} %refs_0_.1, f32[3,64,8,16]{3,2,1,0:T(8,128)} %copy.9.refs_1_, f32[96,64]{1,0:T(8,128)} %constant.12.clone.refs_2_, f32[16,16,768]{2,1,0:T(8,128)} %constant.13.clone.refs_3_, f32[256,128]{1,0:T(8,128)} %constant.14.clone.refs_4_, f32[144,256]{1,0:T(8,128)} %constant.15.clone.refs_5_, ...), custom_call_target="tpu_custom_call" | custom-call | tf_op jit(solution)/shard_map/pallas_call | solution.py:403
  74.6 0.7 copy.11
where the time goes:
time: 75.5 us; the launch traced here: 75.3 us
  Pallas kernels  72.5 us (96%)
  local copies, waits for them, and re-layouts  2.8 us (4%)
    pallas_call x1, Pallas kernels, local(): pl.pallas_call(functools.partial(kernel, gz, gy, nz, yc, xc), out_shape=p...  72.5 us
    unnamed x2, local copies, waits for them, and re-layouts  2.8 us

commit v1 on v0

v1 whole, which is shorter than its diff:
```python
import functools

import jax
import jax.numpy as jnp
import numpy as np
from jax import lax
from jax.experimental import pallas as pl
from jax.experimental.pallas import tpu as pltpu
from jax.sharding import PartitionSpec as P

LANES = 128
INNER = [1.0, 0.0, -5.0 / 4.0, -35.0 / 12.0, 21.0 / 4.0, -25.0 / 12.0]
MIDDLE = [-4.0, 75.0 / 4.0, -245.0 / 8.0, 545.0 / 24.0, -63.0 / 8.0, 25.0 / 24.0]
OUTER = [18.0, -153.0 / 4.0, 255.0 / 8.0, -313.0 / 24.0, 21.0 / 8.0, -5.0 / 24.0]


def shifted(factors, base, slope):
    total = np.polynomial.Polynomial([0.0])
    for factor in reversed(factors):
        total = total * np.polynomial.Polynomial([base, slope]) + factor
    coefs = np.zeros(6)
    coefs[: len(total.coef)] = total.coef
    return [0.0 if abs(c) < 1e-10 else float(c) for c in coefs]


AHEAD = {1: shifted(INNER, 1.0, -1.0), 2: shifted(MIDDLE, 2.0, -1.0), 3: shifted(OUTER, 3.0, -1.0)}
BEHIND = {1: shifted(MIDDLE, 1.0, 1.0), 2: shifted(OUTER, 2.0, 1.0)}


def horner(factors, value):
    lowest = 0
    while factors[lowest] == 0.0:
        lowest += 1
    result = jnp.full_like(value, factors[-1])
    for factor in reversed(factors[lowest:-1]):
        result = result * value
        if factor != 0.0:
            result = result + factor
    for _ in range(lowest):
        result = result * value
    return result


def weights(moved):
    size = jnp.abs(moved)
    positive = moved >= 0.0
    result = {0: horner(INNER, size)}
    for m in (1, 2, 3):
        near = horner(AHEAD[m], size)
        far = horner(BEHIND[m], size) if m in BEHIND else jnp.zeros_like(size)
        result[m] = jnp.where(positive, near, far)
        result[-m] = jnp.where(positive, far, near)
    return result


def displacement(speed, before, after):
    return speed + 0.5 * speed * jnp.where(speed >= 0.0, after - speed, speed - before)


def roll(value, shift, axis):
    return pltpu.roll(value, shift % value.shape[axis], axis)


def sweep_periodic(field, speed, axis):
    moved = displacement(speed, roll(speed, 1, axis), roll(speed, -1, axis))
    w = weights(moved)
    result = field * w[0]
    for m in (-3, -2, -1, 1, 2, 3):
        result = result + roll(field * w[m], m, axis)
    return result


def split(value):
    high = value.astype(jnp.bfloat16)
    return high, (value - high.astype(jnp.float32)).astype(jnp.bfloat16)


def dot(a, b, dims=((1,), (0,))):
    return lax.dot_general(a, b, (dims, ((), ())), preferred_element_type=jnp.float32)


def exact_left(a, value, dims=((1,), (0,))):
    high, low = split(value)
    return dot(a, high, dims) + dot(a, low, dims)


def exact_right(value, b):
    high, low = split(value)
    return dot(high, b) + dot(low, b)


HALO = 3
GROUP = 32


def plan(nz, xc, bc, even):
    first = {True: (0, 0, 0), False: (bc - 1, bc, bc)}[even]
    last = {True: (bc + 2, bc + 1, bc + 1), False: (xc, xc, xc)}[even]
    return [(c, x, nz + (c == 2)) for c in range(3) for x in range(first[c], last[c])]


def side_plan(nz, xc):
    return [(0, xc - 1, nz), (0, 0, nz), (0, 1, nz), (1, 0, nz), (2, 0, nz + 1)]


def positions(entries):
    at, out = 0, []
    for c, x, n in entries:
        out.append((at, c, x, n))
        at += n
    assert at <= LANES
    return out


def constants(nz, gz, gy, yc, xc):
    bc = gz * xc // gy
    bf = 3 * bc
    ny = 3 * gy * yc
    to_xy = np.zeros((2, 2 * LANES, 2 * LANES), np.float32)
    to_z = np.zeros((2, (nz + 1) * bf, 2 * LANES), np.float32)
    for odd in range(2):
        where = {}
        for at, c, x, n in positions(plan(nz, xc, bc, not odd)):
            for i in range(n):
                where[c, x - odd * bc, i] = at + i
        for at, c, x, n in positions(side_plan(nz, xc)):
            col = x + xc - odd * bc if odd else x - xc
            if (c, col, 0) in where or (odd and x == xc - 1) or (not odd and x != xc - 1):
                continue
            for i in range(n):
                where[c, col, i] = LANES + at + i
        for c in range(3):
            reach = range(-HALO, bf + HALO) if c == 0 else range(bf)
            for col in reach:
                k = col % 3
                for rel, weight in ((col // 3, 3 - k), (col // 3 + 1, k)):
                    if weight == 0:
                        continue
                    for i in range(nz + (c == 2)):
                        src = where[c, rel, i]
                        if c == 0:
                            to_xy[odd, src, (GROUP * i + col) % LANES] += weight
                        elif c == 1:
                            to_xy[odd, src, LANES + GROUP * i + col] += weight
                        else:
                            to_z[odd, bf * i + col, src] += weight
    along = np.zeros((gy * yc, ny), np.float32)
    for c in range(gy * yc):
        for k in range(3):
            along[c, 3 * c + k] += 3 - k
            along[(c + 1) % (gy * yc), 3 * c + k] += k
    return to_xy, to_z, along, np.ascontiguousarray(along.T)


def wrapped(index, size):
    return jnp.where(index >= size, index - size, index)


def kernel(gz, gy, nz, yc, xc, *refs):
    (scalar_hbm, vel_hbm, xy_hbm, zz_hbm, ey_hbm, eyt_hbm, out,
     scalar, vel, xy_m, zz_m, ey_m, eyt_m,
     vsend, ssend, vmain, vside, blocks, pencil, edge_out, edge_in,
     up_out, down_out, up_in, down_in,
     local_sem, main_s, main_r, side_s, side_r, blk_s, blk_r, edge_s, z_s, z_r) = refs
    h = lax.axis_index("gz")
    s = lax.axis_index("gy")
    rf = 3 * yc
    bc = gz * xc // gy
    bf = 3 * bc
    total = gz * nz
    nx = scalar.shape[2]
    ny = gy * rf
    odd = lax.rem(s, 2)
    owner = lax.div(s, 2)
    beside = wrapped(owner + jnp.where(odd == 1, 1, gz - 1), gz)
    partner = h + 1 - 2 * lax.rem(h, 2)

    loads = []
    for i, (src, dst) in enumerate((
        (vel_hbm, vel), (scalar_hbm, scalar), (xy_hbm.at[odd], xy_m), (zz_hbm.at[odd], zz_m),
        (ey_hbm, ey_m), (eyt_hbm, eyt_m),
    )):
        load = pltpu.make_async_copy(src, dst, local_sem.at[i])
        load.start()
        loads.append(load)

    barrier = pltpu.get_barrier_semaphore()

    def greet(p, g):
        pl.semaphore_signal(
            barrier, inc=1, device_id={"gz": p, "gy": g}, device_id_type=pl.DeviceIdType.MESH
        )

    for step in range(1, gy):
        g = wrapped(s + step, gy)
        greet(h, g)
        greet(owner, g)
        greet(beside, g)

    @pl.when(owner != h)
    def _():
        greet(owner, s)

    @pl.when(beside != h)
    def _():
        greet(beside, s)

    @pl.when(h > 0)
    def _():
        greet(h - 1, s)

    @pl.when(h < gz - 1)
    def _():
        greet(h + 1, s)

    own = (owner == h).astype(jnp.int32) + (beside == h).astype(jnp.int32)
    ends = (h == 0).astype(jnp.int32) + (h == gz - 1).astype(jnp.int32)

    def remote(src, dst, send, recv, p, g):
        return pltpu.make_async_remote_copy(
            src_ref=src, dst_ref=dst, send_sem=send, recv_sem=recv,
            device_id={"gz": p, "gy": g}, device_id_type=pl.DeviceIdType.MESH,
        )

    loads[0].wait()
    lane = lax.broadcasted_iota(jnp.int32, (yc, LANES), 1)
    row = lax.broadcasted_iota(jnp.int32, (yc, LANES), 0)
    fill = jnp.zeros((yc, LANES - total), jnp.float32)
    source = {
        (c, x): jnp.concatenate([vel[c, :, x, :], fill], axis=1)
        for c in range(3) for x in range(xc)
    }

    def message(entries, p):
        tile = jnp.zeros((yc, LANES), jnp.float32)
        for at, c, x, n in positions(entries):
            z = p * nz - (1 - p % 2 if c == 2 else 0)
            tile = jnp.where(
                (lane >= at) & (lane < at + n), roll(source[c, x], at - z, 1), tile
            )
        return tile

    parts = LANES // GROUP
    for p in range(gz):
        vsend[p, 0] = message(plan(nz, xc, bc, True), p)
        vsend[p, 1] = message(plan(nz, xc, bc, False), p)
        tile = message(side_plan(nz, xc), p)
        wide = tile
        for k in range(1, parts):
            wide = jnp.where(row % parts == k, roll(tile, k * GROUP, 1), wide)
        ssend[p] = jnp.concatenate(
            [jnp.sum(wide[i : i + parts], axis=0, keepdims=True) for i in range(0, yc, parts)],
            axis=0,
        )

    pl.semaphore_wait(barrier, 3 * (gy - 1) + 4 - own - ends)

    def main_copy(p, c, act, own_too):
        g = 2 * h + c
        mine = (p == h) & (g == s)

        @pl.when(jnp.logical_not(mine))
        def _():
            act(remote(vsend.at[p, c], vmain.at[s], main_s.at[2 * p + c], main_r.at[s], p, g))

        if own_too:
            @pl.when(mine)
            def _():
                act(pltpu.make_async_copy(vsend.at[p, c], vmain.at[s], main_r.at[s]))

    def side_copy(p, c, act, own_too):
        g = wrapped(2 * h + (2 if c else gy - 1), gy)
        mine = (p == h) & (g == s)

        @pl.when(jnp.logical_not(mine))
        def _():
            act(remote(ssend.at[p], vside.at[s], side_s.at[2 * p + c], side_r.at[s], p, g))

        if own_too:
            @pl.when(mine)
            def _():
                act(pltpu.make_async_copy(ssend.at[p], vside.at[s], side_r.at[s]))

    tiles = [(p, c) for p in range(gz) for c in range(2)]
    for p, c in tiles:
        main_copy(p, c, lambda copy: copy.start(), True)
    for p, c in tiles:
        side_copy(p, c, lambda copy: copy.start(), True)

    loads[1].wait()
    wide = lax.broadcasted_iota(jnp.int32, (rf, LANES), 1)
    place = [lax.rem(wide + (HALO - GROUP * z) % LANES, LANES) for z in range(nz)]
    for g in range(gy):
        low = g * bf - HALO
        tile = jnp.zeros((rf, LANES), jnp.float32)
        for z in range(nz):
            for t in range(low // LANES, (low + GROUP - 1) // LANES + 1):
                at = t * LANES % nx
                piece = scalar[z, :, at : at + LANES]
                begin = max(0, t * LANES - low)
                end = min(GROUP, (t + 1) * LANES - low)
                tile = jnp.where(
                    (place[z] >= begin) & (place[z] < end),
                    roll(piece, z * GROUP - g * bf, 1),
                    tile,
                )
        blocks[g] = tile

    def block_copy(step):
        g = wrapped(s + step, gy)
        if step == 0:
            return pltpu.make_async_copy(blocks.at[g], pencil.at[s], blk_r.at[s])
        return remote(blocks.at[g], pencil.at[s], blk_s.at[step], blk_r.at[s], h, g)

    sends = [block_copy(step) for step in range(gy)]
    for copy in sends[1:] + sends[:1]:
        copy.start()

    for load in loads[2:]:
        load.wait()
    for i in range(gy):
        pltpu.make_async_copy(vmain.at[i], vmain.at[i], main_r.at[i]).wait()
        pltpu.make_async_copy(vside.at[i], vside.at[i], side_r.at[i]).wait()

    sides = []
    for i in range(gy):
        both = vside[i]
        tall = jnp.where(row < parts, both[0:1], both[1:2])
        tile = tall
        for k in range(1, parts):
            tile = jnp.where(row % parts == k, roll(tall, -k * GROUP, 1), tile)
        sides.append(tile)
    nyc = gy * yc
    coarse = jnp.concatenate(
        [vmain[...].reshape(nyc, LANES), jnp.concatenate(sides, axis=0)], axis=1
    )
    ninth = 1.0 / 9.0
    speed = exact_left(eyt_m[...], exact_right(coarse, xy_m[...])) * ninth
    speed_z = exact_right(exact_left(zz_m[...], coarse, ((1,), (1,))), ey_m[...]) * ninth

    upper = lax.rem(h, 2) == 1
    edge_out[...] = jnp.where(upper, speed_z[:bf], speed_z[nz * bf :])
    edge = remote(edge_out, edge_in, edge_s.at[0], edge_s.at[1], partner, s)
    edge.start()

    for i in range(gy):
        pltpu.make_async_copy(pencil.at[i], pencil.at[i], blk_r.at[i]).wait()
    field = pencil[...].reshape(ny, LANES)
    field = sweep_periodic(field, speed[:, :LANES], 1)
    field = sweep_periodic(field, speed[:, LANES:], 0)

    edge.wait()
    chunks = ny // LANES
    below, above = wrapped(h + gz - 1, gz), wrapped(h + 1, gz)
    ups, downs = [], []
    for k in range(chunks):
        cols = slice(k * LANES, (k + 1) * LANES)
        turned = jnp.transpose(field[cols])
        part = jnp.concatenate([turned[GROUP * z : GROUP * z + bf] for z in range(nz)], axis=0)
        near, far = speed_z[:, cols], edge_in[:, cols]
        six = jnp.concatenate(
            [jnp.where(upper, far, near[:bf]),
             jnp.where(upper, near[: nz * bf], near[bf:]),
             jnp.where(upper, near[nz * bf :], far)], axis=0
        )
        moved = displacement(
            six[bf : (nz + 1) * bf], six[: nz * bf], six[2 * bf :]
        )
        w = weights(moved)

        def landing(target):
            result = None
            for m in range(-3, 4):
                z = target - m
                if 0 <= z < nz:
                    at = slice(z * bf, (z + 1) * bf)
                    term = part[at] * w[m][at]
                    result = term if result is None else result + term
            return result

        for i in range(3):
            up_out[k, i] = landing(nz + i)
            down_out[k, i] = landing(i - 3)
        up = remote(up_out.at[k], up_in.at[k], z_s.at[0, k], z_r.at[0, k], above, s)
        down = remote(down_out.at[k], down_in.at[k], z_s.at[1, k], z_r.at[1, k], below, s)
        ups.append(up)
        downs.append(down)

        @pl.when(h < gz - 1)
        def _():
            up.start()

        @pl.when(h > 0)
        def _():
            down.start()

        for i in range(nz):
            out[i, :, cols] = landing(i)

    @pl.when(h > 0)
    def _():
        for k in range(chunks):
            cols = slice(k * LANES, (k + 1) * LANES)
            ups[k].wait_recv()
            for i in range(3):
                out[i, :, cols] = out[i, :, cols] + up_in[k, i]
        for copy in downs:
            copy.wait_send()

    @pl.when(h < gz - 1)
    def _():
        for k in range(chunks):
            cols = slice(k * LANES, (k + 1) * LANES)
            downs[k].wait_recv()
            for i in range(nz - 3, nz):
                out[i, :, cols] = out[i, :, cols] + down_in[k, i - nz + 3]
        for copy in ups:
            copy.wait_send()

    for copy in sends[1:]:
        copy.wait_send()
    for p, c in tiles:
        main_copy(p, c, lambda copy: copy.wait_send(), False)
        side_copy(p, c, lambda copy: copy.wait_send(), False)


def local(scalar, velocity):
    gz, gy = lax.axis_size("gz"), lax.axis_size("gy")
    nz, rf, nx = scalar.shape
    yc, xc = velocity.shape[2:]
    bc = gz * xc // gy
    bf = 3 * bc
    ny = gy * rf
    mats = [jnp.asarray(m, jnp.bfloat16) for m in constants(nz, gz, gy, yc, xc)]
    turned = jnp.transpose(velocity, (0, 2, 3, 1))
    f32 = jnp.float32
    dma = pltpu.SemaphoreType.DMA
    anywhere = pl.BlockSpec(memory_space=pl.ANY)
    vmem = pl.BlockSpec(memory_space=pltpu.VMEM)
    scratch = [pltpu.VMEM(scalar.shape, f32), pltpu.VMEM(turned.shape, f32)]
    scratch += [pltpu.VMEM(m.shape[1:], jnp.bfloat16) for m in mats[:2]]
    scratch += [pltpu.VMEM(m.shape, jnp.bfloat16) for m in mats[2:]]
    scratch += [
        pltpu.VMEM((gz, 2, yc, LANES), f32),
        pltpu.VMEM((gz, 2, LANES), f32),
        pltpu.VMEM((gy, yc, LANES), f32),
        pltpu.VMEM((gy, 2, LANES), f32),
        pltpu.VMEM((gy, rf, LANES), f32),
        pltpu.VMEM((gy, rf, LANES), f32),
        pltpu.VMEM((bf, ny), f32),
        pltpu.VMEM((bf, ny), f32),
    ]
    scratch += [pltpu.VMEM((ny // LANES, 3, bf, LANES), f32)] * 4
    scratch += [dma((n,)) for n in (2 + len(mats), 2 * gz, gy, 2 * gz, gy, gy, gy, 2)]
    scratch += [dma((2, ny // LANES))] * 2
    return pl.pallas_call(
        functools.partial(kernel, gz, gy, nz, yc, xc),
        out_shape=pltpu.VMEM((nz, bf, ny), f32),
        in_specs=[anywhere] * (2 + len(mats)),
        out_specs=vmem,
        scratch_shapes=scratch,
        compiler_params=pltpu.CompilerParams(has_side_effects=True, collective_id=0),
    )(scalar, turned, *mats)


def solution(mesh):
    in_specs = (P("gz", "gy", None), P(None, None, "gy", "gz"))
    out_specs = P("gz", "gy", None)
    return jax.shard_map(local, mesh=mesh, in_specs=in_specs, out_specs=out_specs, check_vma=False)
```

time: 75.5 us -> 55.7 us (0.74)
  the two profiles are of different devices: /device:TPU:1 before, /device:TPU:53 now
where the time goes in v1:
time: 55.7 us; the launch traced here: 55.6 us
  Pallas kernels  54.9 us (99%)
  local copies, waits for them, and re-layouts  0.72 us (1%)
    pallas_call x1, Pallas kernels, local(): pl.pallas_call(functools.partial(kernel, gz, gy, nz, yc, xc), out_shape=p...  54.9 us

profile of v1, /device:TPU:53, one launch (start us, length us, event | category | flops | bytes accessed | tf_op | source)
XLA Modules:
  0.0 55.6 jit_solution(8543593616126713918)
XLA Ops:
  0.0 54.9 %shard_map.64 = f32[4,24,768]{2,1,0:T(8,128)S(1)} custom-call(f32[4,24,768]{2,1,0:T(8,128)} %refs_0_.1, f32[3,8,16,64]{3,2,1,0:T(8,128)} %bitcast.1, bf16[2,256,256]{2,1,0:T(8,128)(2,1)} %constant.8.clone.refs_2_, bf16[2,120,256]{2,1,0:T(8,128)(2,1)} %constant.9.clone.refs_3_, bf16[256,768]{1,0:T(8,128)(2,1)} %constant.10.clone.refs_4_, ...), custom_call_target="tpu_custom_call" | custom-call | tf_op jit(solution)/shard_map/pallas_call | solution.py:456
  54.9 0.7 %copy.8 = f32[4,24,768]{2,1,0:T(8,128)} copy(f32[4,24,768]{2,1,0:T(8,128)S(1)} %shard_map.64) | data formatting | bytes 589824

commit v2 on v1

--- a/solution.py
+++ b/solution.py
@@ -90,6 +90,7 @@
 
 
 HALO = 3
+EDGE = 8
 GROUP = 32
 
 
@@ -159,9 +160,10 @@
 def kernel(gz, gy, nz, yc, xc, *refs):
     (scalar_hbm, vel_hbm, xy_hbm, zz_hbm, ey_hbm, eyt_hbm, out,
      scalar, vel, xy_m, zz_m, ey_m, eyt_m,
-     vsend, ssend, vmain, vside, blocks, pencil, edge_out, edge_in,
+     vsend, ssend, vmain, vside, blocks, pencil, after, speed_y, turned_z, edge_out, edge_in,
      up_out, down_out, up_in, down_in,
-     local_sem, main_s, main_r, side_s, side_r, blk_s, blk_r, edge_s, z_s, z_r) = refs
+     local_sem, main_s, main_r, side_s, side_r, blk_s, blk_r, edge_s, z_s, z_r,
+     ready_b, ready_v, ready_z) = refs
     h = lax.axis_index("gz")
     s = lax.axis_index("gy")
     rf = 3 * yc
@@ -191,30 +193,76 @@
             barrier, inc=1, device_id={"gz": p, "gy": g}, device_id_type=pl.DeviceIdType.MESH
         )
 
-    for step in range(1, gy):
-        g = wrapped(s + step, gy)
+    def flag(condition):
+        return jnp.where(condition, 1, 0)
+
+    reach = [wrapped(2 * h + (j - 1 if j else gy - 1), gy) for j in range(4)]
+
+    def greet_higher(g, _):
         greet(h, g)
         greet(owner, g)
         greet(beside, g)
-
-    @pl.when(owner != h)
+        return 0
+
+    lax.fori_loop(s + 1, gy, greet_higher, 0)
+
+    def higher_targets(g, act):
+        def one(q, _):
+            act(q)
+            return 0
+
+        lax.fori_loop(jnp.where(g > s, 0, jnp.where(g == s, h + 1, gz)), gz, one, 0)
+
+    for g in reach:
+        higher_targets(g, lambda q, g=g: greet(q, g))
+
+    @pl.when(owner > h)
     def _():
         greet(owner, s)
 
-    @pl.when(beside != h)
+    @pl.when(beside > h)
     def _():
         greet(beside, s)
 
+    @pl.when(h < gz - 1)
+    def _():
+        greet(h + 1, s)
+
+    lower = 3 * s + flag(owner < h) + flag(beside < h) + flag(h > 0)
+    for g in reach:
+        lower = lower + jnp.where(g < s, gz, jnp.where(g == s, h, 0))
+
+    @pl.when(lower > 0)
+    def _():
+        pl.semaphore_wait(barrier, lower)
+
+    def tell(semaphore, p, g):
+        pl.semaphore_signal(
+            semaphore, inc=1, device_id={"gz": p, "gy": g}, device_id_type=pl.DeviceIdType.MESH
+        )
+
+    from_owner = ready_v.at[4 * h + 1 + odd]
+    from_beside = ready_v.at[4 * h + 3 - 3 * odd]
+
+    def tell_lower(g, _):
+        tell(ready_b.at[s], h, g)
+        tell(from_owner, owner, g)
+        tell(from_beside, beside, g)
+        return 0
+
+    lax.fori_loop(0, s, tell_lower, 0)
+
+    @pl.when(owner < h)
+    def _():
+        tell(from_owner, owner, s)
+
+    @pl.when(beside < h)
+    def _():
+        tell(from_beside, beside, s)
+
     @pl.when(h > 0)
     def _():
-        greet(h - 1, s)
-
-    @pl.when(h < gz - 1)
-    def _():
-        greet(h + 1, s)
-
-    own = (owner == h).astype(jnp.int32) + (beside == h).astype(jnp.int32)
-    ends = (h == 0).astype(jnp.int32) + (h == gz - 1).astype(jnp.int32)
+        tell(ready_z, h - 1, s)
 
     def remote(src, dst, send, recv, p, g):
         return pltpu.make_async_remote_copy(
@@ -235,10 +283,8 @@
         tile = jnp.zeros((yc, LANES), jnp.float32)
         for at, c, x, n in positions(entries):
             z = p * nz - (1 - p % 2 if c == 2 else 0)
-            tile = jnp.where(
-                (lane >= at) & (lane < at + n), roll(source[c, x], at - z, 1), tile
-            )
-        return tile
+            tile = jnp.where(lane >= at, roll(source[c, x], at - z, 1), tile)
+        return jnp.where(lane < at + n, tile, 0.0)
 
     parts = LANES // GROUP
     for p in range(gz):
@@ -253,8 +299,6 @@
             axis=0,
         )
 
-    pl.semaphore_wait(barrier, 3 * (gy - 1) + 4 - own - ends)
-
     def main_copy(p, c, act, own_too):
         g = 2 * h + c
         mine = (p == h) & (g == s)
@@ -282,10 +326,20 @@
                 act(pltpu.make_async_copy(ssend.at[p], vside.at[s], side_r.at[s]))
 
     tiles = [(p, c) for p in range(gz) for c in range(2)]
-    for p, c in tiles:
-        main_copy(p, c, lambda copy: copy.start(), True)
-    for p, c in tiles:
-        side_copy(p, c, lambda copy: copy.start(), True)
+
+    def send_velocity():
+        for j in (1, 2, 0, 3):
+            higher_targets(reach[j], lambda q, j=j: pl.semaphore_wait(ready_v.at[4 * q + j], 1))
+            for p in range(gz):
+                (main_copy if j in (1, 2) else side_copy)(
+                    p, j - 1 if j in (1, 2) else j // 3, lambda copy: copy.start(), True
+                )
+
+    soon = 2 * h + 1 < s
+
+    @pl.when(soon)
+    def _():
+        send_velocity()
 
     loads[1].wait()
     wide = lax.broadcasted_iota(jnp.int32, (rf, LANES), 1)
@@ -307,14 +361,23 @@
         blocks[g] = tile
 
     def block_copy(step):
-        g = wrapped(s + step, gy)
+        g = jnp.where(step <= s, s - step, step)
         if step == 0:
             return pltpu.make_async_copy(blocks.at[g], pencil.at[s], blk_r.at[s])
         return remote(blocks.at[g], pencil.at[s], blk_s.at[step], blk_r.at[s], h, g)
 
     sends = [block_copy(step) for step in range(gy)]
-    for copy in sends[1:] + sends[:1]:
-        copy.start()
+    sends[0].start()
+    for step in range(1, gy):
+        @pl.when(step > s)
+        def _():
+            pl.semaphore_wait(ready_b.at[step], 1)
+
+        sends[step].start()
+
+    @pl.when(jnp.logical_not(soon))
+    def _():
+        send_velocity()
 
     for load in loads[2:]:
         load.wait()
@@ -336,18 +399,32 @@
     )
     ninth = 1.0 / 9.0
     speed = exact_left(eyt_m[...], exact_right(coarse, xy_m[...])) * ninth
-    speed_z = exact_right(exact_left(zz_m[...], coarse, ((1,), (1,))), ey_m[...]) * ninth
+    speed_y[EDGE : EDGE + ny] = speed[:, LANES:]
+    speed_y[:EDGE] = speed[ny - EDGE :, LANES:]
+    speed_y[EDGE + ny :] = speed[:EDGE, LANES:]
+    turned_z[...] = exact_right(exact_left(zz_m[...], coarse, ((1,), (1,))), ey_m[...]) * ninth
 
     upper = lax.rem(h, 2) == 1
-    edge_out[...] = jnp.where(upper, speed_z[:bf], speed_z[nz * bf :])
+    edge_out[...] = jnp.where(upper, turned_z[:bf], turned_z[nz * bf :])
     edge = remote(edge_out, edge_in, edge_s.at[0], edge_s.at[1], partner, s)
+
+    @pl.when(h < gz - 1)
+    def _():
+        pl.semaphore_wait(ready_z, 1)
+
     edge.start()
 
     for i in range(gy):
         pltpu.make_async_copy(pencil.at[i], pencil.at[i], blk_r.at[i]).wait()
-    field = pencil[...].reshape(ny, LANES)
-    field = sweep_periodic(field, speed[:, :LANES], 1)
-    field = sweep_periodic(field, speed[:, LANES:], 0)
+    joined = 4
+    for i in range(0, gy, joined):
+        rows = slice(i * rf, (i + joined) * rf)
+        field = pencil[i : i + joined].reshape(joined * rf, LANES)
+        after[EDGE + i * rf : EDGE + (i + joined) * rf] = sweep_periodic(
+            field, speed[rows, :LANES], 1
+        )
+    after[:EDGE] = after[ny : ny + EDGE]
+    after[EDGE + ny :] = after[EDGE : 2 * EDGE]
 
     edge.wait()
     chunks = ny // LANES
@@ -355,9 +432,11 @@
     ups, downs = [], []
     for k in range(chunks):
         cols = slice(k * LANES, (k + 1) * LANES)
-        turned = jnp.transpose(field[cols])
+        rows = slice(k * LANES, (k + 1) * LANES + 2 * EDGE)
+        swept = sweep_periodic(after[rows], speed_y[rows], 0)
+        turned = jnp.transpose(swept[EDGE : EDGE + LANES])
         part = jnp.concatenate([turned[GROUP * z : GROUP * z + bf] for z in range(nz)], axis=0)
-        near, far = speed_z[:, cols], edge_in[:, cols]
+        near, far = turned_z[:, cols], edge_in[:, cols]
         six = jnp.concatenate(
             [jnp.where(upper, far, near[:bf]),
              jnp.where(upper, near[: nz * bf], near[bf:]),
@@ -447,12 +526,17 @@
         pltpu.VMEM((gy, 2, LANES), f32),
         pltpu.VMEM((gy, rf, LANES), f32),
         pltpu.VMEM((gy, rf, LANES), f32),
+        pltpu.VMEM((ny + 2 * EDGE, LANES), f32),
+        pltpu.VMEM((ny + 2 * EDGE, LANES), f32),
+        pltpu.VMEM(((nz + 1) * bf, ny), f32),
         pltpu.VMEM((bf, ny), f32),
         pltpu.VMEM((bf, ny), f32),
     ]
     scratch += [pltpu.VMEM((ny // LANES, 3, bf, LANES), f32)] * 4
     scratch += [dma((n,)) for n in (2 + len(mats), 2 * gz, gy, 2 * gz, gy, gy, gy, 2)]
     scratch += [dma((2, ny // LANES))] * 2
+    regular = pltpu.SemaphoreType.REGULAR
+    scratch += [regular((gy,)), regular((4 * gz,)), regular]
     return pl.pallas_call(
         functools.partial(kernel, gz, gy, nz, yc, xc),
         out_shape=pltpu.VMEM((nz, bf, ny), f32),

time: 55.7 us -> 58.6 us (1.052)
  the two profiles are of different devices: /device:TPU:53 before, /device:TPU:5 now
where the time goes in v2:
time: 58.6 us; the launch traced here: 58.5 us
  Pallas kernels  57.8 us (99%)
  local copies, waits for them, and re-layouts  0.72 us (1%)
    pallas_call x1, Pallas kernels, local(): pl.pallas_call(functools.partial(kernel, gz, gy, nz, yc, xc), out_shape=p...  57.8 us

profile of v2, /device:TPU:5, one launch (start us, length us, event | category | flops | bytes accessed | tf_op | source)
XLA Modules:
  0.0 58.5 jit_solution(9718831527627873989)
XLA Ops:
  0.0 57.8 %shard_map.64 = f32[4,24,768]{2,1,0:T(8,128)S(1)} custom-call(f32[4,24,768]{2,1,0:T(8,128)} %refs_0_.1, f32[3,8,16,64]{3,2,1,0:T(8,128)} %bitcast.1, bf16[2,256,256]{2,1,0:T(8,128)(2,1)} %constant.8.clone.refs_2_, bf16[2,120,256]{2,1,0:T(8,128)(2,1)} %constant.9.clone.refs_3_, bf16[256,768]{1,0:T(8,128)(2,1)} %constant.10.clone.refs_4_, ...), custom_call_target="tpu_custom_call" | custom-call | tf_op jit(solution)/shard_map/pallas_call | solution.py:540
  57.8 0.7 %copy.8 = f32[4,24,768]{2,1,0:T(8,128)} copy(f32[4,24,768]{2,1,0:T(8,128)S(1)} %shard_map.64) | data formatting | bytes 589824

commit v3 on v0

v3 whole, which is shorter than its diff:
```python
import functools

import jax
import jax.numpy as jnp
import numpy as np
from jax import lax
from jax.experimental import pallas as pl
from jax.experimental.pallas import tpu as pltpu
from jax.sharding import PartitionSpec as P

LANES = 128
INNER = [1.0, 0.0, -5.0 / 4.0, -35.0 / 12.0, 21.0 / 4.0, -25.0 / 12.0]
MIDDLE = [-4.0, 75.0 / 4.0, -245.0 / 8.0, 545.0 / 24.0, -63.0 / 8.0, 25.0 / 24.0]
OUTER = [18.0, -153.0 / 4.0, 255.0 / 8.0, -313.0 / 24.0, 21.0 / 8.0, -5.0 / 24.0]


def shifted(factors, base, slope):
    total = np.polynomial.Polynomial([0.0])
    for factor in reversed(factors):
        total = total * np.polynomial.Polynomial([base, slope]) + factor
    coefs = np.zeros(6)
    coefs[: len(total.coef)] = total.coef
    return [0.0 if abs(c) < 1e-10 else float(c) for c in coefs]


AHEAD = {1: shifted(INNER, 1.0, -1.0), 2: shifted(MIDDLE, 2.0, -1.0), 3: shifted(OUTER, 3.0, -1.0)}
BEHIND = {1: shifted(MIDDLE, 1.0, 1.0), 2: shifted(OUTER, 2.0, 1.0)}


def horner(factors, value):
    lowest = 0
    while factors[lowest] == 0.0:
        lowest += 1
    result = jnp.full_like(value, factors[-1])
    for factor in reversed(factors[lowest:-1]):
        result = result * value
        if factor != 0.0:
            result = result + factor
    for _ in range(lowest):
        result = result * value
    return result


def weights(moved):
    size = jnp.abs(moved)
    positive = moved >= 0.0
    result = {0: horner(INNER, size)}
    for m in (1, 2, 3):
        near = horner(AHEAD[m], size)
        far = horner(BEHIND[m], size) if m in BEHIND else jnp.zeros_like(size)
        result[m] = jnp.where(positive, near, far)
        result[-m] = jnp.where(positive, far, near)
    return result


def displacement(speed, before, after):
    return speed + 0.5 * speed * jnp.where(speed >= 0.0, after - speed, speed - before)


def roll(value, shift, axis):
    return pltpu.roll(value, shift % value.shape[axis], axis)


def sweep_periodic(field, speed, axis):
    moved = displacement(speed, roll(speed, 1, axis), roll(speed, -1, axis))
    w = weights(moved)
    result = field * w[0]
    for m in (-3, -2, -1, 1, 2, 3):
        result = result + roll(field * w[m], m, axis)
    return result


def split(value):
    high = value.astype(jnp.bfloat16)
    return high, (value - high.astype(jnp.float32)).astype(jnp.bfloat16)


def dot(a, b, dims=((1,), (0,))):
    return lax.dot_general(a, b, (dims, ((), ())), preferred_element_type=jnp.float32)


def exact_left(a, value, dims=((1,), (0,))):
    high, low = split(value)
    return dot(a, high, dims) + dot(a, low, dims)


def exact_right(value, b):
    high, low = split(value)
    return dot(high, b) + dot(low, b)


EDGE = 8
NINTH = 1.0 / 9.0


def along(count):
    out = np.zeros((count, 3 * count), np.float32)
    for c in range(count):
        for k in range(3):
            out[c, 3 * c + k] += 3 - k
            out[(c + 1) % count, 3 * c + k] += k
    return out


def constants(nz, gz, gy, yc, xc):
    bc = gz * xc // gy
    bf = 3 * bc
    rf = 3 * yc
    spare = LANES - nz * bf
    rows = np.zeros((nz * rf, nz * yc + 8), np.float32)
    for z in range(nz):
        for r in range(rf):
            y, k = divmod(r, 3)
            rows[z * rf + r, z * yc + y] += 3 - k
            rows[z * rf + r, z * yc + y + 1 if y < yc - 1 else nz * yc + z] += k
    groups = rf // yc
    to_y = np.zeros((groups * LANES, LANES), np.float32)
    to_z = np.zeros(((nz + 2) * bf, groups * LANES), np.float32)
    for plane in range(2 * nz + 2):
        for c in range(bf):
            for col, weight in ((c // 3, 3 - c % 3), (c // 3 + 1, c % 3)):
                if weight == 0:
                    continue
                group, at = divmod(plane * (bc + 1) + col, spare)
                src = group * LANES + nz * bf + at
                if plane < nz:
                    to_y[src, plane * bf + c] += weight
                else:
                    to_z[(plane - nz) * bf + c, src] += weight
    ey = along(gy * yc)
    return rows, along(gz * xc), to_y, to_z, ey, np.ascontiguousarray(ey.T)


def wrapped(index, size):
    return jnp.where(index >= size, index - size, index)


def kernel(gz, gy, nz, yc, xc, *refs):
    (scalar_hbm, vel_hbm, rows_hbm, ex_hbm, yy_hbm, zz_hbm, ey_hbm, eyt_hbm, out,
     scalar, vel, rows_m, ex_m, yy_m, zz_m, ey_m, eyt_m,
     xsend, wsend, own, nxt, other, blocks, pencil, speed_y,
     up_out, down_out, up_in, down_in,
     local_sem, own_s, own_r, nxt_s, nxt_r, oth_s, oth_r, blk_s, blk_r, z_s, z_r, ready) = refs
    h = lax.axis_index("gz")
    s = lax.axis_index("gy")
    rf = 3 * yc
    bc = gz * xc // gy
    bf = 3 * bc
    total = gz * nz
    nx = scalar.shape[2]
    ny = gy * rf
    behind, ahead = wrapped(s + gy - 1, gy), wrapped(s + 1, gy)

    loads = []
    for i, (src, dst) in enumerate((
        (vel_hbm, vel), (scalar_hbm, scalar), (rows_hbm, rows_m), (ex_hbm, ex_m),
        (yy_hbm, yy_m), (zz_hbm, zz_m), (ey_hbm, ey_m), (eyt_hbm, eyt_m),
    )):
        load = pltpu.make_async_copy(src, dst, local_sem.at[i])
        load.start()
        loads.append(load)

    barrier = pltpu.get_barrier_semaphore()

    def tell(semaphore, p, g):
        pl.semaphore_signal(
            semaphore, inc=1, device_id={"gz": p, "gy": g}, device_id_type=pl.DeviceIdType.MESH
        )

    def each(low, high, act):
        def one(i, _):
            act(i)
            return 0

        lax.fori_loop(low, high, one, 0)

    for step in range(1, gz):
        tell(barrier, wrapped(h + step, gz), s)
    for step in range(gz):
        tell(barrier, wrapped(h + step, gz), ahead)
    each(s + 1, gy, lambda g: tell(barrier, h, g))

    def remote(src, dst, send, recv, p, g):
        return pltpu.make_async_remote_copy(
            src_ref=src, dst_ref=dst, send_sem=send, recv_sem=recv,
            device_id={"gz": p, "gy": g}, device_id_type=pl.DeviceIdType.MESH,
        )

    loads[0].wait()
    fill = jnp.zeros((yc * xc, LANES - total), jnp.float32)

    def by_plane(c):
        wide = jnp.concatenate([vel[c].reshape(yc * xc, total), fill], axis=1)
        return jnp.transpose(wide)

    planes = by_plane(0)
    for p in range(gz):
        xsend[p] = planes[p * nz : (p + 1) * nz]
    planes = by_plane(1)
    for p in range(gz):
        wsend[p, :nz] = planes[p * nz : (p + 1) * nz]
    planes = by_plane(2)
    for p in range(gz):
        if p == 0:
            wsend[p, nz : nz + 1] = jnp.zeros((1, LANES), jnp.float32)
            wsend[p, nz + 1 :] = planes[: nz + 1]
        else:
            wsend[p, nz:] = planes[p * nz - 1 : (p + 1) * nz + 1]

    pl.semaphore_wait(barrier, 2 * gz - 1 + s)

    firsts, nexts, others = [], [], []
    for step in range(gz):
        p = wrapped(h + step, gz)
        if step:
            firsts.append(remote(xsend.at[p], own.at[h], own_s.at[step], own_r.at[h], p, s))
            others.append(remote(wsend.at[p], other.at[h], oth_s.at[step], oth_r.at[h], p, s))
        else:
            firsts.append(pltpu.make_async_copy(xsend.at[p], own.at[h], own_r.at[h]))
            others.append(pltpu.make_async_copy(wsend.at[p], other.at[h], oth_r.at[h]))
        nexts.append(remote(xsend.at[p], nxt.at[h], nxt_s.at[step], nxt_r.at[h], p, behind))
    for first, following in zip(firsts, nexts):
        first.start()
        following.start()
    for copy in others:
        copy.start()
    each(0, s, lambda g: tell(ready.at[s], h, g))

    lane = lax.broadcasted_iota(jnp.int32, (yc, LANES), 1)
    row = lax.broadcasted_iota(jnp.int32, (yc, LANES), 0)
    block = lane // xc

    def swap(value):
        for k in (1, 2, 4):
            row_bit, lane_bit = (row // k) % 2, (block // k) % 2
            value = jnp.where(
                row_bit == lane_bit,
                value,
                jnp.where(
                    row_bit == 0,
                    roll(roll(value, -k, 0), k * xc, 1),
                    roll(roll(value, k, 0), -k * xc, 1),
                ),
            )
        return value

    def spread(value):
        value = jnp.where(lane < xc, value, 0.0)
        for k in (1, 2, 4):
            value = jnp.where((row // k) % 2 == 1, roll(value, k * xc, 1), value)
        return jnp.sum(value, axis=0, keepdims=True)

    halves = [slice(i, i + yc) for i in range(0, gz, yc)]
    for i in range(gz):
        pltpu.make_async_copy(own.at[i], own.at[i], own_r.at[i]).wait()
        pltpu.make_async_copy(nxt.at[i], nxt.at[i], nxt_r.at[i]).wait()
    coarse = []
    for source, act in ((own, swap), (nxt, spread)):
        for z in range(nz):
            value = source[:, z, :]
            coarse.append(jnp.concatenate([act(value[half]) for half in halves], axis=1))
    coarse.append(jnp.zeros((8 - nz, gz * xc), jnp.float32))
    coarse = jnp.concatenate(coarse, axis=0)
    for load in loads[1:4]:
        load.wait()
    speed = exact_right(exact_left(rows_m[...], coarse), ex_m[...]) * NINTH
    field = scalar[...].reshape(nz * rf, nx)
    field = sweep_periodic(field, speed, 1)

    for i in range(gz):
        pltpu.make_async_copy(other.at[i], other.at[i], oth_r.at[i]).wait()
    kept = [[swap(other[:, k, :][half]) for half in halves] for k in range(2 * nz + 2)]
    wide = lax.broadcasted_iota(jnp.int32, (rf, LANES), 1)
    spare = LANES - nz * bf
    for g in range(gy):
        low = g * bf
        tile = None
        for z in range(nz):
            for t in range(low // LANES, (low + bf - 1) // LANES + 1):
                piece = field[z * rf : (z + 1) * rf, t * LANES : (t + 1) * LANES]
                begin = z * bf + max(0, t * LANES - low)
                moved = roll(piece, z * bf - low, 1)
                tile = moved if tile is None else jnp.where(wide >= begin, moved, tile)
        flat = jnp.zeros((yc, LANES), jnp.float32)
        for k in range(2 * nz + 2):
            at = k * (bc + 1)
            first = g * bc
            t, begin = divmod(first, LANES)
            flat = jnp.where(lane >= at, roll(kept[k][t], at - begin, 1), flat)
            if begin + bc == LANES:
                t = (t + 1) % len(halves)
                flat = jnp.where(lane >= at + bc, roll(kept[k][t], at + bc, 1), flat)
        flat = jnp.where(lane < (2 * nz + 2) * (bc + 1), flat, 0.0)
        extra = jnp.concatenate(
            [roll(flat, nz * bf - i * spare, 1) for i in range(rf // yc)], axis=0
        )
        blocks[g] = jnp.where(wide >= nz * bf, extra, tile)

    def block_copy(step):
        g = jnp.where(step <= s, s - step, step)
        if step == 0:
            return pltpu.make_async_copy(blocks.at[g], pencil.at[s], blk_r.at[s])
        return remote(blocks.at[g], pencil.at[s], blk_s.at[step], blk_r.at[s], h, g)

    sends = [block_copy(step) for step in range(gy)]
    sends[0].start()
    for step in range(1, gy):
        @pl.when(step > s)
        def _():
            pl.semaphore_wait(ready.at[step], 1)

        sends[step].start()

    for load in loads[4:]:
        load.wait()
    for i in range(gy):
        pltpu.make_async_copy(pencil.at[i], pencil.at[i], blk_r.at[i]).wait()
    nyc = gy * yc
    coarse = jnp.concatenate(
        [pencil[:, i : i + yc, :].reshape(nyc, LANES) for i in range(0, rf, yc)], axis=1
    )
    speed = exact_left(eyt_m[...], exact_right(coarse, yy_m[...])) * NINTH
    speed_y[EDGE : EDGE + ny] = speed
    speed_y[:EDGE] = speed[ny - EDGE :]
    speed_y[EDGE + ny :] = speed[:EDGE]
    speed_z = exact_right(exact_left(zz_m[...], coarse, ((1,), (1,))), ey_m[...]) * NINTH

    chunks = ny // LANES
    below, above = wrapped(h + gz - 1, gz), wrapped(h + 1, gz)
    whole = pencil[...].reshape(ny, LANES)
    around = jnp.concatenate([whole[ny - EDGE :], whole, whole[:EDGE]], axis=0)
    ups, downs = [], []
    for k in range(chunks):
        cols = slice(k * LANES, (k + 1) * LANES)
        rows = slice(k * LANES, (k + 1) * LANES + 2 * EDGE)
        swept = sweep_periodic(around[rows], speed_y[rows], 0)
        part = jnp.transpose(swept[EDGE : EDGE + LANES])[: nz * bf]
        moved = displacement(
            speed_z[bf : (nz + 1) * bf, cols], speed_z[: nz * bf, cols], speed_z[2 * bf :, cols]
        )
        w = weights(moved)

        def landing(target):
            result = None
            for m in range(-3, 4):
                z = target - m
                if 0 <= z < nz:
                    at = slice(z * bf, (z + 1) * bf)
                    term = part[at] * w[m][at]
                    result = term if result is None else result + term
            return result

        for i in range(3):
            up_out[k, i] = landing(nz + i)
            down_out[k, i] = landing(i - 3)
        up = remote(up_out.at[k], up_in.at[k], z_s.at[0, k], z_r.at[0, k], above, s)
        down = remote(down_out.at[k], down_in.at[k], z_s.at[1, k], z_r.at[1, k], below, s)
        ups.append(up)
        downs.append(down)

        @pl.when(h < gz - 1)
        def _():
            up.start()

        @pl.when(h > 0)
        def _():
            down.start()

        for i in range(nz):
            out[i, :, cols] = landing(i)

    @pl.when(h > 0)
    def _():
        for k in range(chunks):
            cols = slice(k * LANES, (k + 1) * LANES)
            ups[k].wait_recv()
            for i in range(3):
                out[i, :, cols] = out[i, :, cols] + up_in[k, i]
        for copy in downs:
            copy.wait_send()

    @pl.when(h < gz - 1)
    def _():
        for k in range(chunks):
            cols = slice(k * LANES, (k + 1) * LANES)
            downs[k].wait_recv()
            for i in range(nz - 3, nz):
                out[i, :, cols] = out[i, :, cols] + down_in[k, i - nz + 3]
        for copy in ups:
            copy.wait_send()

    for copy in sends[1:] + firsts[1:] + nexts + others[1:]:
        copy.wait_send()


def local(scalar, velocity):
    gz, gy = lax.axis_size("gz"), lax.axis_size("gy")
    nz, rf, nx = scalar.shape
    yc, xc = velocity.shape[2:]
    bc = gz * xc // gy
    bf = 3 * bc
    ny = gy * rf
    mats = [jnp.asarray(m, jnp.bfloat16) for m in constants(nz, gz, gy, yc, xc)]
    turned = jnp.transpose(velocity, (0, 2, 3, 1))
    f32 = jnp.float32
    dma = pltpu.SemaphoreType.DMA
    anywhere = pl.BlockSpec(memory_space=pl.ANY)
    vmem = pl.BlockSpec(memory_space=pltpu.VMEM)
    scratch = [pltpu.VMEM(scalar.shape, f32), pltpu.VMEM(turned.shape, f32)]
    scratch += [pltpu.VMEM(m.shape, jnp.bfloat16) for m in mats]
    scratch += [
        pltpu.VMEM((gz, nz, LANES), f32),
        pltpu.VMEM((gz, 2 * nz + 2, LANES), f32),
        pltpu.VMEM((gz, nz, LANES), f32),
        pltpu.VMEM((gz, nz, LANES), f32),
        pltpu.VMEM((gz, 2 * nz + 2, LANES), f32),
        pltpu.VMEM((gy, rf, LANES), f32),
        pltpu.VMEM((gy, rf, LANES), f32),
        pltpu.VMEM((ny + 2 * EDGE, LANES), f32),
    ]
    scratch += [pltpu.VMEM((ny // LANES, 3, bf, LANES), f32)] * 4
    scratch += [dma((n,)) for n in (2 + len(mats), gz, gz, gz, gz, gz, gz, gy, gy)]
    scratch += [dma((2, ny // LANES))] * 2
    scratch += [pltpu.SemaphoreType.REGULAR((gy,))]
    return pl.pallas_call(
        functools.partial(kernel, gz, gy, nz, yc, xc),
        out_shape=pltpu.VMEM((nz, bf, ny), f32),
        in_specs=[anywhere] * (2 + len(mats)),
        out_specs=vmem,
        scratch_shapes=scratch,
        compiler_params=pltpu.CompilerParams(has_side_effects=True, collective_id=0),
    )(scalar, turned, *mats)


def solution(mesh):
    in_specs = (P("gz", "gy", None), P(None, None, "gy", "gz"))
    out_specs = P("gz", "gy", None)
    return jax.shard_map(local, mesh=mesh, in_specs=in_specs, out_specs=out_specs, check_vma=False)
```

time: 75.5 us -> 54.5 us (0.72)
  the two profiles are of different devices: /device:TPU:1 before, /device:TPU:9 now
where the time goes in v3:
time: 54.5 us; the launch traced here: 54.4 us
  Pallas kernels  53.7 us (99%)
  local copies, waits for them, and re-layouts  0.72 us (1%)
    pallas_call x1, Pallas kernels, local(): pl.pallas_call(functools.partial(kernel, gz, gy, nz, yc, xc), out_shape=p...  53.7 us

profile of v3, /device:TPU:9, one launch (start us, length us, event | category | flops | bytes accessed | tf_op | source)
XLA Modules:
  0.0 54.4 jit_solution(16268883029039704612)
XLA Ops:
  0.0 53.7 %shard_map.82 = f32[4,24,768]{2,1,0:T(8,128)S(1)} custom-call(f32[4,24,768]{2,1,0:T(8,128)} %refs_0_.1, f32[3,8,16,64]{3,2,1,0:T(8,128)} %bitcast.1, bf16[96,40]{1,0:T(8,128)(2,1)} %constant.10.clone.refs_2_, bf16[256,768]{1,0:T(8,128)(2,1)} %constant.11.clone.refs_3_.refs_6_, bf16[384,128]{1,0:T(8,128)(2,1)} %constant.12.clone.refs_4_, ...), custom_call_target="tpu_custom_call" | custom-call | tf_op jit(solution)/shard_map/pallas_call | solution.py:425
  53.7 0.7 %copy.10 = f32[4,24,768]{2,1,0:T(8,128)} copy(f32[4,24,768]{2,1,0:T(8,128)S(1)} %shard_map.82) | data formatting | bytes 589824

commit v4 on v3

--- a/solution.py
+++ b/solution.py
@@ -90,6 +90,18 @@
 
 
 EDGE = 8
+REACH = 4
+SPAN = 8
+
+
+def touched(chunk, yc):
+    first, end = chunk * LANES - REACH, (chunk + 1) * LANES + REACH
+    low = min((first // 3) // yc, (chunk * LANES - EDGE) // (3 * yc))
+    high = max(((end - 1) // 3 + 1) // yc, ((chunk + 1) * LANES + EDGE - 1) // (3 * yc))
+    assert high - low < SPAN
+    return low, high
+
+
 NINTH = 1.0 / 9.0
 
 
@@ -127,8 +139,19 @@
                     to_y[src, plane * bf + c] += weight
                 else:
                     to_z[(plane - nz) * bf + c, src] += weight
-    ey = along(gy * yc)
-    return rows, along(gz * xc), to_y, to_z, ey, np.ascontiguousarray(ey.T)
+    chunks = gy * rf // LANES
+    down = np.zeros((chunks, LANES + 2 * EDGE, SPAN * yc), np.float32)
+    across = np.zeros((chunks, SPAN * yc, LANES), np.float32)
+    for chunk in range(chunks):
+        base = yc * touched(chunk, yc)[0]
+        for r in range(-REACH, LANES + REACH):
+            c, k = divmod(chunk * LANES + r, 3)
+            for at, weight in ((c - base, 3 - k), (c + 1 - base, k)):
+                if weight:
+                    down[chunk, EDGE + r, at] += weight
+                    if 0 <= r < LANES:
+                        across[chunk, at, r] += weight
+    return rows, along(gz * xc), to_y, to_z, across, down
 
 
 def wrapped(index, size):
@@ -138,7 +161,7 @@
 def kernel(gz, gy, nz, yc, xc, *refs):
     (scalar_hbm, vel_hbm, rows_hbm, ex_hbm, yy_hbm, zz_hbm, ey_hbm, eyt_hbm, out,
      scalar, vel, rows_m, ex_m, yy_m, zz_m, ey_m, eyt_m,
-     xsend, wsend, own, nxt, other, blocks, pencil, speed_y,
+     xsend, wsend, own, nxt, other, kept, blocks, pencil,
      up_out, down_out, up_in, down_in,
      local_sem, own_s, own_r, nxt_s, nxt_r, oth_s, oth_r, blk_s, blk_r, z_s, z_r, ready) = refs
     h = lax.axis_index("gz")
@@ -266,77 +289,107 @@
     speed = exact_right(exact_left(rows_m[...], coarse), ex_m[...]) * NINTH
     field = scalar[...].reshape(nz * rf, nx)
     field = sweep_periodic(field, speed, 1)
+    for z in range(nz):
+        scalar[z] = field[z * rf : (z + 1) * rf]
 
     for i in range(gz):
         pltpu.make_async_copy(other.at[i], other.at[i], oth_r.at[i]).wait()
-    kept = [[swap(other[:, k, :][half]) for half in halves] for k in range(2 * nz + 2)]
+    for k in range(2 * nz + 2):
+        parts = [swap(other[:, k, :][half]) for half in halves]
+        for t, part in enumerate(parts + parts[:1]):
+            kept[k, :, t * LANES : (t + 1) * LANES] = part
     wide = lax.broadcasted_iota(jnp.int32, (rf, LANES), 1)
     spare = LANES - nz * bf
-    for g in range(gy):
+    last = nx // LANES - 1
+
+    def build(step):
+        g = jnp.where(step <= s, s - step, step)
         low = g * bf
+        t = lax.div(low, LANES)
+        here = pl.ds(pl.multiple_of(t * LANES, LANES), LANES)
+        there = pl.ds(pl.multiple_of(jnp.minimum(t + 1, last) * LANES, LANES), LANES)
         tile = None
         for z in range(nz):
-            for t in range(low // LANES, (low + bf - 1) // LANES + 1):
-                piece = field[z * rf : (z + 1) * rf, t * LANES : (t + 1) * LANES]
-                begin = z * bf + max(0, t * LANES - low)
-                moved = roll(piece, z * bf - low, 1)
-                tile = moved if tile is None else jnp.where(wide >= begin, moved, tile)
-        flat = jnp.zeros((yc, LANES), jnp.float32)
+            piece = jnp.where(
+                wide < low + bf - (t + 1) * LANES, scalar[z, :, there], scalar[z, :, here]
+            )
+            piece = pltpu.roll(piece, lax.rem(z * bf + nx - low, LANES), 1)
+            tile = piece if tile is None else jnp.where(wide >= z * bf, piece, tile)
+        first = g * bc
+        t = lax.div(first, LANES)
+        here = pl.ds(pl.multiple_of(t * LANES, LANES), LANES)
+        there = pl.ds(pl.multiple_of((t + 1) * LANES, LANES), LANES)
+        flat = None
         for k in range(2 * nz + 2):
             at = k * (bc + 1)
-            first = g * bc
-            t, begin = divmod(first, LANES)
-            flat = jnp.where(lane >= at, roll(kept[k][t], at - begin, 1), flat)
-            if begin + bc == LANES:
-                t = (t + 1) % len(halves)
-                flat = jnp.where(lane >= at + bc, roll(kept[k][t], at + bc, 1), flat)
+            piece = jnp.where(
+                lane < first + bc + 1 - (t + 1) * LANES, kept[k, :, there], kept[k, :, here]
+            )
+            piece = pltpu.roll(piece, lax.rem(at + nx - first, LANES), 1)
+            flat = piece if flat is None else jnp.where(lane >= at, piece, flat)
         flat = jnp.where(lane < (2 * nz + 2) * (bc + 1), flat, 0.0)
         extra = jnp.concatenate(
             [roll(flat, nz * bf - i * spare, 1) for i in range(rf // yc)], axis=0
         )
-        blocks[g] = jnp.where(wide >= nz * bf, extra, tile)
+        blocks[step] = jnp.where(wide >= nz * bf, extra, tile)
 
     def block_copy(step):
         g = jnp.where(step <= s, s - step, step)
-        if step == 0:
-            return pltpu.make_async_copy(blocks.at[g], pencil.at[s], blk_r.at[s])
-        return remote(blocks.at[g], pencil.at[s], blk_s.at[step], blk_r.at[s], h, g)
-
-    sends = [block_copy(step) for step in range(gy)]
-    sends[0].start()
-    for step in range(1, gy):
+        return remote(blocks.at[step], pencil.at[s], blk_s.at[step], blk_r.at[s], h, g)
+
+    def send(step):
         @pl.when(step > s)
         def _():
             pl.semaphore_wait(ready.at[step], 1)
 
-        sends[step].start()
+        block_copy(step).start()
+
+    def pair(i):
+        build(2 * i + 1)
+        build(2 * i + 2)
+        send(2 * i + 1)
+        send(2 * i + 2)
+
+    each(0, gy // 2 - 1, pair)
+    build(gy - 1)
+    send(gy - 1)
+    build(0)
+    pltpu.make_async_copy(blocks.at[0], pencil.at[s], blk_r.at[s]).start()
 
     for load in loads[4:]:
         load.wait()
-    for i in range(gy):
-        pltpu.make_async_copy(pencil.at[i], pencil.at[i], blk_r.at[i]).wait()
-    nyc = gy * yc
-    coarse = jnp.concatenate(
-        [pencil[:, i : i + yc, :].reshape(nyc, LANES) for i in range(0, rf, yc)], axis=1
-    )
-    speed = exact_left(eyt_m[...], exact_right(coarse, yy_m[...])) * NINTH
-    speed_y[EDGE : EDGE + ny] = speed
-    speed_y[:EDGE] = speed[ny - EDGE :]
-    speed_y[EDGE + ny :] = speed[:EDGE]
-    speed_z = exact_right(exact_left(zz_m[...], coarse, ((1,), (1,))), ey_m[...]) * NINTH
-
     chunks = ny // LANES
+    order = list(range(1, chunks)) + [0]
+    here = set()
     below, above = wrapped(h + gz - 1, gz), wrapped(h + 1, gz)
-    whole = pencil[...].reshape(ny, LANES)
-    around = jnp.concatenate([whole[ny - EDGE :], whole, whole[:EDGE]], axis=0)
-    ups, downs = [], []
-    for k in range(chunks):
+    ups, downs = {}, {}
+    for k in order:
         cols = slice(k * LANES, (k + 1) * LANES)
-        rows = slice(k * LANES, (k + 1) * LANES + 2 * EDGE)
-        swept = sweep_periodic(around[rows], speed_y[rows], 0)
+        low, high = touched(k, yc)
+        gs = [g % gy for g in range(low, high + 1)]
+        for g in gs:
+            if g not in here:
+                here.add(g)
+                pltpu.make_async_copy(pencil.at[g], pencil.at[g], blk_r.at[g]).wait()
+        got = jnp.concatenate([pencil[g] for g in gs], axis=0)
+        coarse = [
+            jnp.concatenate([pencil[g, i : i + yc, :] for g in gs], axis=0)
+            for i in range(0, rf, yc)
+        ]
+        coarse = jnp.concatenate(coarse, axis=1)
+        if len(gs) < SPAN:
+            coarse = jnp.concatenate(
+                [coarse, jnp.zeros(((SPAN - len(gs)) * yc, coarse.shape[1]), jnp.float32)], axis=0
+            )
+        for_y = exact_right(coarse, yy_m[...])
+        for_z = exact_left(zz_m[...], coarse, ((1,), (1,)))
+        speed_y = exact_left(eyt_m[k], for_y) * NINTH
+        speed_z = exact_right(for_z, ey_m[k]) * NINTH
+        start = k * LANES - EDGE - low * rf
+        swept = sweep_periodic(got[start : start + LANES + 2 * EDGE], speed_y, 0)
         part = jnp.transpose(swept[EDGE : EDGE + LANES])[: nz * bf]
         moved = displacement(
-            speed_z[bf : (nz + 1) * bf, cols], speed_z[: nz * bf, cols], speed_z[2 * bf :, cols]
+            speed_z[bf : (nz + 1) * bf], speed_z[: nz * bf], speed_z[2 * bf :]
         )
         w = weights(moved)
 
@@ -355,8 +408,7 @@
             down_out[k, i] = landing(i - 3)
         up = remote(up_out.at[k], up_in.at[k], z_s.at[0, k], z_r.at[0, k], above, s)
         down = remote(down_out.at[k], down_in.at[k], z_s.at[1, k], z_r.at[1, k], below, s)
-        ups.append(up)
-        downs.append(down)
+        ups[k], downs[k] = up, down
 
         @pl.when(h < gz - 1)
         def _():
@@ -371,26 +423,27 @@
 
     @pl.when(h > 0)
     def _():
-        for k in range(chunks):
+        for k in order:
             cols = slice(k * LANES, (k + 1) * LANES)
             ups[k].wait_recv()
             for i in range(3):
                 out[i, :, cols] = out[i, :, cols] + up_in[k, i]
-        for copy in downs:
+        for copy in downs.values():
             copy.wait_send()
 
     @pl.when(h < gz - 1)
     def _():
-        for k in range(chunks):
+        for k in order:
             cols = slice(k * LANES, (k + 1) * LANES)
             downs[k].wait_recv()
             for i in range(nz - 3, nz):
                 out[i, :, cols] = out[i, :, cols] + down_in[k, i - nz + 3]
-        for copy in ups:
+        for copy in ups.values():
             copy.wait_send()
 
-    for copy in sends[1:] + firsts[1:] + nexts + others[1:]:
+    for copy in firsts[1:] + nexts + others[1:]:
         copy.wait_send()
+    each(1, gy, lambda step: block_copy(step).wait_send())
 
 
 def local(scalar, velocity):
@@ -414,9 +467,9 @@
         pltpu.VMEM((gz, nz, LANES), f32),
         pltpu.VMEM((gz, nz, LANES), f32),
         pltpu.VMEM((gz, 2 * nz + 2, LANES), f32),
+        pltpu.VMEM((2 * nz + 2, yc, gz * xc + LANES), f32),
         pltpu.VMEM((gy, rf, LANES), f32),
         pltpu.VMEM((gy, rf, LANES), f32),
-        pltpu.VMEM((ny + 2 * EDGE, LANES), f32),
     ]
     scratch += [pltpu.VMEM((ny // LANES, 3, bf, LANES), f32)] * 4
     scratch += [dma((n,)) for n in (2 + len(mats), gz, gz, gz, gz, gz, gz, gy, gy)]

time: 54.5 us -> 48.7 us (0.89)
  the two profiles are of different devices: /device:TPU:9 before, /device:TPU:1 now
where the time goes in v4:
time: 48.7 us; the launch traced here: 48.4 us
  Pallas kernels  47.7 us (98%)
  local copies, waits for them, and re-layouts  0.72 us (1%)
    pallas_call x1, Pallas kernels, local(): pl.pallas_call(functools.partial(kernel, gz, gy, nz, yc, xc), out_shape=p...  47.7 us

profile of v4, /device:TPU:1, one launch (start us, length us, event | category | flops | bytes accessed | tf_op | source)
XLA Modules:
  0.0 48.4 jit_solution(18265292048773333167)
XLA Ops:
  0.0 47.7 %shard_map.82 = f32[4,24,768]{2,1,0:T(8,128)S(1)} custom-call(f32[4,24,768]{2,1,0:T(8,128)} %refs_0_.1, f32[3,8,16,64]{3,2,1,0:T(8,128)} %bitcast.1, bf16[96,40]{1,0:T(8,128)(2,1)} %constant.12.clone.refs_2_, bf16[256,768]{1,0:T(8,128)(2,1)} %constant.13.clone.refs_3_, bf16[384,128]{1,0:T(8,128)(2,1)} %constant.14.clone.refs_4_, ...), custom_call_target="tpu_custom_call" | custom-call | tf_op jit(solution)/shard_map/pallas_call | solution.py:478
  47.7 0.7 %copy.10 = f32[4,24,768]{2,1,0:T(8,128)} copy(f32[4,24,768]{2,1,0:T(8,128)S(1)} %shard_map.82) | data formatting | bytes 589824

commit v5 on v4

--- a/solution.py
+++ b/solution.py
@@ -91,13 +91,24 @@
 
 EDGE = 8
 REACH = 4
-SPAN = 8
-
-
-def touched(chunk, yc):
-    first, end = chunk * LANES - REACH, (chunk + 1) * LANES + REACH
-    low = min((first // 3) // yc, (chunk * LANES - EDGE) // (3 * yc))
-    high = max(((end - 1) // 3 + 1) // yc, ((chunk + 1) * LANES + EDGE - 1) // (3 * yc))
+SPAN = 24
+TURN = 4
+WIDTHS = (1, 1, 1, 3)
+
+
+def windows(chunks):
+    out, at = [], 1
+    while at <= chunks:
+        width = min(WIDTHS[len(out) % len(WIDTHS)], chunks + 1 - at)
+        out.append((at, width))
+        at += width
+    return out
+
+
+def touched(chunk, width, yc):
+    first, end = chunk * LANES, (chunk + width) * LANES
+    low = min(((first - REACH) // 3) // yc, (first - EDGE) // (3 * yc))
+    high = max(((end + REACH - 1) // 3 + 1) // yc, (end + EDGE - 1) // (3 * yc))
     assert high - low < SPAN
     return low, high
 
@@ -139,18 +150,19 @@
                     to_y[src, plane * bf + c] += weight
                 else:
                     to_z[(plane - nz) * bf + c, src] += weight
-    chunks = gy * rf // LANES
-    down = np.zeros((chunks, LANES + 2 * EDGE, SPAN * yc), np.float32)
-    across = np.zeros((chunks, SPAN * yc, LANES), np.float32)
-    for chunk in range(chunks):
-        base = yc * touched(chunk, yc)[0]
-        for r in range(-REACH, LANES + REACH):
+    parts = windows(gy * rf // LANES)
+    most = LANES * max(width for _, width in parts)
+    down = np.zeros((len(parts), most + 2 * EDGE, SPAN * yc), np.float32)
+    across = np.zeros((len(parts), SPAN * yc, most), np.float32)
+    for i, (chunk, width) in enumerate(parts):
+        base = yc * touched(chunk, width, yc)[0]
+        for r in range(-REACH, width * LANES + REACH):
             c, k = divmod(chunk * LANES + r, 3)
             for at, weight in ((c - base, 3 - k), (c + 1 - base, k)):
                 if weight:
-                    down[chunk, EDGE + r, at] += weight
-                    if 0 <= r < LANES:
-                        across[chunk, at, r] += weight
+                    down[i, EDGE + r, at] += weight
+                    if 0 <= r < width * LANES:
+                        across[i, at, r] += weight
     return rows, along(gz * xc), to_y, to_z, across, down
 
 
@@ -161,7 +173,7 @@
 def kernel(gz, gy, nz, yc, xc, *refs):
     (scalar_hbm, vel_hbm, rows_hbm, ex_hbm, yy_hbm, zz_hbm, ey_hbm, eyt_hbm, out,
      scalar, vel, rows_m, ex_m, yy_m, zz_m, ey_m, eyt_m,
-     xsend, wsend, own, nxt, other, kept, blocks, pencil,
+     xsend, nsend, wsend, own, nxt, other, kept, blocks, pencil,
      up_out, down_out, up_in, down_in,
      local_sem, own_s, own_r, nxt_s, nxt_r, oth_s, oth_r, blk_s, blk_r, z_s, z_r, ready) = refs
     h = lax.axis_index("gz")
@@ -219,6 +231,14 @@
     planes = by_plane(0)
     for p in range(gz):
         xsend[p] = planes[p * nz : (p + 1) * nz]
+    tall = lax.broadcasted_iota(jnp.int32, (LANES, LANES), 0)
+    bottom = jnp.where(lax.broadcasted_iota(jnp.int32, (LANES, LANES), 1) < xc, planes, 0.0)
+    shifts = [roll(bottom, i * xc, 1) if i else bottom for i in range(nz)]
+    bottom = shifts[0]
+    for i in range(1, nz):
+        bottom = jnp.where(tall % nz == i, shifts[i], bottom)
+    for p in range(gz):
+        nsend[p] = jnp.sum(bottom[p * nz : (p + 1) * nz], axis=0, keepdims=True)
     planes = by_plane(1)
     for p in range(gz):
         wsend[p, :nz] = planes[p * nz : (p + 1) * nz]
@@ -241,11 +261,8 @@
         else:
             firsts.append(pltpu.make_async_copy(xsend.at[p], own.at[h], own_r.at[h]))
             others.append(pltpu.make_async_copy(wsend.at[p], other.at[h], oth_r.at[h]))
-        nexts.append(remote(xsend.at[p], nxt.at[h], nxt_s.at[step], nxt_r.at[h], p, behind))
-    for first, following in zip(firsts, nexts):
-        first.start()
-        following.start()
-    for copy in others:
+        nexts.append(remote(nsend.at[p], nxt.at[h], nxt_s.at[step], nxt_r.at[h], p, behind))
+    for copy in firsts + nexts + others:
         copy.start()
     each(0, s, lambda g: tell(ready.at[s], h, g))
 
@@ -267,22 +284,13 @@
             )
         return value
 
-    def spread(value):
-        value = jnp.where(lane < xc, value, 0.0)
-        for k in (1, 2, 4):
-            value = jnp.where((row // k) % 2 == 1, roll(value, k * xc, 1), value)
-        return jnp.sum(value, axis=0, keepdims=True)
-
     halves = [slice(i, i + yc) for i in range(0, gz, yc)]
     for i in range(gz):
         pltpu.make_async_copy(own.at[i], own.at[i], own_r.at[i]).wait()
         pltpu.make_async_copy(nxt.at[i], nxt.at[i], nxt_r.at[i]).wait()
     coarse = []
-    for source, act in ((own, swap), (nxt, spread)):
-        for z in range(nz):
-            value = source[:, z, :]
-            coarse.append(jnp.concatenate([act(value[half]) for half in halves], axis=1))
-    coarse.append(jnp.zeros((8 - nz, gz * xc), jnp.float32))
+    for value in [own[:, z, :] for z in range(nz)] + [nxt[:, 0, :]]:
+        coarse.append(jnp.concatenate([swap(value[half]) for half in halves], axis=1))
     coarse = jnp.concatenate(coarse, axis=0)
     for load in loads[1:4]:
         load.wait()
@@ -302,8 +310,12 @@
     spare = LANES - nz * bf
     last = nx // LANES - 1
 
+    def target(step):
+        near = jnp.where(step <= s, s - step, step)
+        return jnp.where(s >= 3 * gy // 4, wrapped(s + step, gy), near)
+
     def build(step):
-        g = jnp.where(step <= s, s - step, step)
+        g = target(step)
         low = g * bf
         t = lax.div(low, LANES)
         here = pl.ds(pl.multiple_of(t * LANES, LANES), LANES)
@@ -334,38 +346,42 @@
         blocks[step] = jnp.where(wide >= nz * bf, extra, tile)
 
     def block_copy(step):
-        g = jnp.where(step <= s, s - step, step)
+        g = target(step)
         return remote(blocks.at[step], pencil.at[s], blk_s.at[step], blk_r.at[s], h, g)
 
     def send(step):
-        @pl.when(step > s)
+        g = target(step)
+
+        @pl.when(g > s)
         def _():
-            pl.semaphore_wait(ready.at[step], 1)
+            pl.semaphore_wait(ready.at[g], 1)
 
         block_copy(step).start()
 
-    def pair(i):
-        build(2 * i + 1)
-        build(2 * i + 2)
-        send(2 * i + 1)
-        send(2 * i + 2)
-
-    each(0, gy // 2 - 1, pair)
-    build(gy - 1)
-    send(gy - 1)
+    def several(i):
+        for j in range(TURN):
+            build(TURN * i + j + 1)
+        for j in range(TURN):
+            send(TURN * i + j + 1)
+
+    turns = (gy - 1) // TURN
+    each(0, turns, several)
+    for step in range(turns * TURN + 1, gy):
+        build(step)
     build(0)
+    for step in range(turns * TURN + 1, gy):
+        send(step)
     pltpu.make_async_copy(blocks.at[0], pencil.at[s], blk_r.at[s]).start()
 
     for load in loads[4:]:
         load.wait()
     chunks = ny // LANES
-    order = list(range(1, chunks)) + [0]
+    order = [k % chunks for chunk, width in windows(chunks) for k in range(chunk, chunk + width)]
     here = set()
     below, above = wrapped(h + gz - 1, gz), wrapped(h + 1, gz)
     ups, downs = {}, {}
-    for k in order:
-        cols = slice(k * LANES, (k + 1) * LANES)
-        low, high = touched(k, yc)
+    for i, (chunk, width) in enumerate(windows(chunks)):
+        low, high = touched(chunk, width, yc)
         gs = [g % gy for g in range(low, high + 1)]
         for g in gs:
             if g not in here:
@@ -373,77 +389,89 @@
                 pltpu.make_async_copy(pencil.at[g], pencil.at[g], blk_r.at[g]).wait()
         got = jnp.concatenate([pencil[g] for g in gs], axis=0)
         coarse = [
-            jnp.concatenate([pencil[g, i : i + yc, :] for g in gs], axis=0)
-            for i in range(0, rf, yc)
+            jnp.concatenate([pencil[g, at : at + yc, :] for g in gs], axis=0)
+            for at in range(0, rf, yc)
         ]
         coarse = jnp.concatenate(coarse, axis=1)
-        if len(gs) < SPAN:
+        span = -(-len(gs) // 8) * 8
+        if len(gs) < span:
             coarse = jnp.concatenate(
-                [coarse, jnp.zeros(((SPAN - len(gs)) * yc, coarse.shape[1]), jnp.float32)], axis=0
+                [coarse, jnp.zeros(((span - len(gs)) * yc, coarse.shape[1]), jnp.float32)], axis=0
             )
         for_y = exact_right(coarse, yy_m[...])
         for_z = exact_left(zz_m[...], coarse, ((1,), (1,)))
-        speed_y = exact_left(eyt_m[k], for_y) * NINTH
-        speed_z = exact_right(for_z, ey_m[k]) * NINTH
-        start = k * LANES - EDGE - low * rf
-        swept = sweep_periodic(got[start : start + LANES + 2 * EDGE], speed_y, 0)
-        part = jnp.transpose(swept[EDGE : EDGE + LANES])[: nz * bf]
-        moved = displacement(
-            speed_z[bf : (nz + 1) * bf], speed_z[: nz * bf], speed_z[2 * bf :]
-        )
-        w = weights(moved)
-
-        def landing(target):
-            result = None
-            for m in range(-3, 4):
-                z = target - m
-                if 0 <= z < nz:
-                    at = slice(z * bf, (z + 1) * bf)
-                    term = part[at] * w[m][at]
-                    result = term if result is None else result + term
-            return result
-
-        for i in range(3):
-            up_out[k, i] = landing(nz + i)
-            down_out[k, i] = landing(i - 3)
-        up = remote(up_out.at[k], up_in.at[k], z_s.at[0, k], z_r.at[0, k], above, s)
-        down = remote(down_out.at[k], down_in.at[k], z_s.at[1, k], z_r.at[1, k], below, s)
-        ups[k], downs[k] = up, down
+        count = width * LANES
+        speed_y = exact_left(eyt_m[i, : count + 2 * EDGE, : span * yc], for_y) * NINTH
+        speed_zs = exact_right(for_z, ey_m[i, : span * yc, :count]) * NINTH
+        start = chunk * LANES - EDGE - low * rf
+        swept = sweep_periodic(got[start : start + count + 2 * EDGE], speed_y, 0)
+        for j in range(width):
+            k = (chunk + j) % chunks
+            cols = slice(k * LANES, (k + 1) * LANES)
+            speed_z = speed_zs[:, j * LANES : (j + 1) * LANES]
+            at = EDGE + j * LANES
+            part = jnp.transpose(swept[at : at + LANES])[: nz * bf]
+            moved = displacement(
+                speed_z[bf : (nz + 1) * bf], speed_z[: nz * bf], speed_z[2 * bf :]
+            )
+            w = weights(moved)
+
+            def landing(target):
+                result = None
+                for m in range(-3, 4):
+                    z = target - m
+                    if 0 <= z < nz:
+                        at = slice(z * bf, (z + 1) * bf)
+                        term = part[at] * w[m][at]
+                        result = term if result is None else result + term
+                return result
+
+            for t in range(3):
+                up_out[k, t] = landing(nz + t)
+                down_out[k, t] = landing(t - 3)
+            for t in range(nz):
+                out[t, :, cols] = landing(t)
+            ups[k] = remote(up_out.at[k], up_in.at[k], z_s.at[0, k], z_r.at[0, k], above, s)
+            downs[k] = remote(down_out.at[k], down_in.at[k], z_s.at[1, k], z_r.at[1, k], below, s)
 
         @pl.when(h < gz - 1)
         def _():
-            up.start()
+            for j in range(width):
+                ups[(chunk + j) % chunks].start()
 
         @pl.when(h > 0)
         def _():
-            down.start()
-
-        for i in range(nz):
-            out[i, :, cols] = landing(i)
-
-    @pl.when(h > 0)
-    def _():
-        for k in order:
-            cols = slice(k * LANES, (k + 1) * LANES)
+            for j in range(width):
+                downs[(chunk + j) % chunks].start()
+
+    for copy in firsts[1:] + nexts + others[1:]:
+        copy.wait_send()
+    each(1, gy, lambda step: block_copy(step).wait_send())
+
+    for k in order:
+        cols = slice(k * LANES, (k + 1) * LANES)
+
+        @pl.when(h > 0)
+        def _():
             ups[k].wait_recv()
             for i in range(3):
                 out[i, :, cols] = out[i, :, cols] + up_in[k, i]
-        for copy in downs.values():
-            copy.wait_send()
-
-    @pl.when(h < gz - 1)
-    def _():
-        for k in order:
-            cols = slice(k * LANES, (k + 1) * LANES)
+
+        @pl.when(h < gz - 1)
+        def _():
             downs[k].wait_recv()
             for i in range(nz - 3, nz):
                 out[i, :, cols] = out[i, :, cols] + down_in[k, i - nz + 3]
+
+    @pl.when(h > 0)
+    def _():
+        for copy in downs.values():
+            copy.wait_send()
+
+    @pl.when(h < gz - 1)
+    def _():
         for copy in ups.values():
             copy.wait_send()
-
-    for copy in firsts[1:] + nexts + others[1:]:
-        copy.wait_send()
-    each(1, gy, lambda step: block_copy(step).wait_send())
 
 
 def local(scalar, velocity):
@@ -463,9 +491,10 @@
     scratch += [pltpu.VMEM(m.shape, jnp.bfloat16) for m in mats]
     scratch += [
         pltpu.VMEM((gz, nz, LANES), f32),
+        pltpu.VMEM((gz, 1, LANES), f32),
         pltpu.VMEM((gz, 2 * nz + 2, LANES), f32),
         pltpu.VMEM((gz, nz, LANES), f32),
-        pltpu.VMEM((gz, nz, LANES), f32),
+        pltpu.VMEM((gz, 1, LANES), f32),
         pltpu.VMEM((gz, 2 * nz + 2, LANES), f32),
         pltpu.VMEM((2 * nz + 2, yc, gz * xc + LANES), f32),
         pltpu.VMEM((gy, rf, LANES), f32),

time: 48.7 us -> 47.9 us (0.984)
  Pallas kernels: 47.7 us -> 47.1 us
    pallas_call x1, Pallas kernels: 47.7 us -> 47.1 us  [local(): pl.pallas_call(functools.partial(kernel, gz, gy, nz, yc, xc), out_shape=p...]
where the time goes in v5:
time: 47.9 us; the launch traced here: 47.8 us
  Pallas kernels  47.1 us (98%)
  local copies, waits for them, and re-layouts  0.72 us (2%)
    pallas_call x1, Pallas kernels, local(): pl.pallas_call(functools.partial(kernel, gz, gy, nz, yc, xc), out_shape=p...  47.1 us

profile of v5, /device:TPU:1, one launch (start us, length us, event | category | flops | bytes accessed | tf_op | source)
XLA Modules:
  0.0 47.8 jit_solution(14858359889738216514)
XLA Ops:
  0.0 47.1 %shard_map.82 = f32[4,24,768]{2,1,0:T(8,128)S(1)} custom-call(f32[4,24,768]{2,1,0:T(8,128)} %refs_0_.1, f32[3,8,16,64]{3,2,1,0:T(8,128)} %bitcast.1, bf16[96,40]{1,0:T(8,128)(2,1)} %constant.12.clone.refs_2_, bf16[256,768]{1,0:T(8,128)(2,1)} %constant.13.clone.refs_3_, bf16[384,128]{1,0:T(8,128)(2,1)} %constant.14.clone.refs_4_, ...), custom_call_target="tpu_custom_call" | custom-call | tf_op jit(solution)/shard_map/pallas_call | solution.py:507
  47.1 0.7 %copy.10 = f32[4,24,768]{2,1,0:T(8,128)} copy(f32[4,24,768]{2,1,0:T(8,128)S(1)} %shard_map.82) | data formatting | bytes 589824

commit v6 on v5

--- a/solution.py
+++ b/solution.py
@@ -9,8 +9,6 @@
 from jax.sharding import PartitionSpec as P
 
 LANES = 128
-INNER = [1.0, 0.0, -5.0 / 4.0, -35.0 / 12.0, 21.0 / 4.0, -25.0 / 12.0]
-MIDDLE = [-4.0, 75.0 / 4.0, -245.0 / 8.0, 545.0 / 24.0, -63.0 / 8.0, 25.0 / 24.0]
 OUTER = [18.0, -153.0 / 4.0, 255.0 / 8.0, -313.0 / 24.0, 21.0 / 8.0, -5.0 / 24.0]
 
 
@@ -23,8 +21,7 @@
     return [0.0 if abs(c) < 1e-10 else float(c) for c in coefs]
 
 
-AHEAD = {1: shifted(INNER, 1.0, -1.0), 2: shifted(MIDDLE, 2.0, -1.0), 3: shifted(OUTER, 3.0, -1.0)}
-BEHIND = {1: shifted(MIDDLE, 1.0, 1.0), 2: shifted(OUTER, 2.0, 1.0)}
+OUTERMOST = shifted(OUTER, 3.0, -1.0)
 
 
 def horner(factors, value):
@@ -42,15 +39,23 @@
 
 
 def weights(moved):
-    size = jnp.abs(moved)
     positive = moved >= 0.0
-    result = {0: horner(INNER, size)}
-    for m in (1, 2, 3):
-        near = horner(AHEAD[m], size)
-        far = horner(BEHIND[m], size) if m in BEHIND else jnp.zeros_like(size)
-        result[m] = jnp.where(positive, near, far)
-        result[-m] = jnp.where(positive, far, near)
-    return result
+    square = moved * moved
+    last = horner(OUTERMOST, jnp.abs(moved))
+    five, ten = 5.0 * last, 10.0 * last
+    inner, outer = square - 1.0, square - 4.0
+    near = moved * outer * (-1.0 / 6.0)
+    far = moved * inner * (1.0 / 24.0)
+    near_even, far_even, far_odd = near * moved, far * moved, far + far
+    return {
+        0: inner * outer * 0.25 - ten,
+        1: near_even + near + jnp.where(positive, ten, five),
+        -1: near_even - near + jnp.where(positive, five, ten),
+        2: far_even + far_odd - jnp.where(positive, five, last),
+        -2: far_even - far_odd - jnp.where(positive, last, five),
+        3: jnp.where(positive, last, 0.0),
+        -3: jnp.where(positive, 0.0, last),
+    }
 
 
 def displacement(speed, before, after):
@@ -298,52 +303,50 @@
     field = scalar[...].reshape(nz * rf, nx)
     field = sweep_periodic(field, speed, 1)
     for z in range(nz):
-        scalar[z] = field[z * rf : (z + 1) * rf]
+        plane = field[z * rf : (z + 1) * rf]
+        scalar[z] = roll(plane, z * bf, 1) if z else plane
 
     for i in range(gz):
         pltpu.make_async_copy(other.at[i], other.at[i], oth_r.at[i]).wait()
     for k in range(2 * nz + 2):
         parts = [swap(other[:, k, :][half]) for half in halves]
-        for t, part in enumerate(parts + parts[:1]):
-            kept[k, :, t * LANES : (t + 1) * LANES] = part
-    wide = lax.broadcasted_iota(jnp.int32, (rf, LANES), 1)
+        row_of = jnp.concatenate(parts, axis=1)
+        kept[k] = roll(row_of, k * (bc + 1), 1) if k else row_of
     spare = LANES - nz * bf
-    last = nx // LANES - 1
+
+    def place(first, count):
+        t = lax.div(first, LANES)
+        off = first - t * LANES
+        tiles = [
+            pl.ds(pl.multiple_of(lax.rem(t + i, count) * LANES, LANES), LANES) for i in range(2)
+        ]
+        return tiles, off, jnp.where(lane < off, lane - off + LANES, lane - off)
 
     def target(step):
+        some = gy // 8
         near = jnp.where(step <= s, s - step, step)
-        return jnp.where(s >= 3 * gy // 4, wrapped(s + step, gy), near)
+        late = jnp.where(step <= s, s + some - step, step)
+        late = jnp.where(step <= some, lax.rem(s + step, some), late)
+        return jnp.where((s >= gy // 2) & (step > 0), late, near)
 
     def build(step):
         g = target(step)
-        low = g * bf
-        t = lax.div(low, LANES)
-        here = pl.ds(pl.multiple_of(t * LANES, LANES), LANES)
-        there = pl.ds(pl.multiple_of(jnp.minimum(t + 1, last) * LANES, LANES), LANES)
-        tile = None
-        for z in range(nz):
-            piece = jnp.where(
-                wide < low + bf - (t + 1) * LANES, scalar[z, :, there], scalar[z, :, here]
-            )
-            piece = pltpu.roll(piece, lax.rem(z * bf + nx - low, LANES), 1)
-            tile = piece if tile is None else jnp.where(wide >= z * bf, piece, tile)
-        first = g * bc
-        t = lax.div(first, LANES)
-        here = pl.ds(pl.multiple_of(t * LANES, LANES), LANES)
-        there = pl.ds(pl.multiple_of((t + 1) * LANES, LANES), LANES)
+        (here, there), off, at = place(g * bf, nx // LANES)
+        (kept_here, kept_there), kept_off, kept_at = place(g * bc, gz * xc // LANES)
         flat = None
         for k in range(2 * nz + 2):
-            at = k * (bc + 1)
-            piece = jnp.where(
-                lane < first + bc + 1 - (t + 1) * LANES, kept[k, :, there], kept[k, :, here]
-            )
-            piece = pltpu.roll(piece, lax.rem(at + nx - first, LANES), 1)
-            flat = piece if flat is None else jnp.where(lane >= at, piece, flat)
-        flat = jnp.where(lane < (2 * nz + 2) * (bc + 1), flat, 0.0)
-        extra = jnp.concatenate(
-            [roll(flat, nz * bf - i * spare, 1) for i in range(rf // yc)], axis=0
-        )
-        blocks[step] = jnp.where(wide >= nz * bf, extra, tile)
+            piece = jnp.where(lane < kept_off, kept[k, :, kept_there], kept[k, :, kept_here])
+            flat = piece if flat is None else jnp.where(kept_at >= k * (bc + 1), piece, flat)
+        flat = jnp.where(kept_at < (2 * nz + 2) * (bc + 1), flat, 0.0)
+        for i in range(rf // yc):
+            rows = slice(i * yc, (i + 1) * yc)
+            tile = None
+            for z in range(nz):
+                piece = jnp.where(lane < off, scalar[z, rows, there], scalar[z, rows, here])
+                tile = piece if tile is None else jnp.where(at >= z * bf, piece, tile)
+            tile = pltpu.roll(tile, lax.rem(LANES - off, LANES), 1)
+            extra = pltpu.roll(flat, lax.rem(LANES + nz * bf - i * spare - kept_off, LANES), 1)
+            blocks[step, rows] = jnp.where(lane >= nz * bf, extra, tile)
 
     def block_copy(step):
         g = target(step)
@@ -496,7 +499,7 @@
         pltpu.VMEM((gz, nz, LANES), f32),
         pltpu.VMEM((gz, 1, LANES), f32),
         pltpu.VMEM((gz, 2 * nz + 2, LANES), f32),
-        pltpu.VMEM((2 * nz + 2, yc, gz * xc + LANES), f32),
+        pltpu.VMEM((2 * nz + 2, yc, gz * xc), f32),
         pltpu.VMEM((gy, rf, LANES), f32),
         pltpu.VMEM((gy, rf, LANES), f32),
     ]

time: 47.9 us -> 47.1 us (0.983)
  the two profiles are of different devices: /device:TPU:1 before, /device:TPU:73 now
where the time goes in v6:
time: 47.1 us; the launch traced here: 47 us
  Pallas kernels  46.3 us (98%)
  local copies, waits for them, and re-layouts  0.72 us (2%)
    pallas_call x1, Pallas kernels, local(): pl.pallas_call(functools.partial(kernel, gz, gy, nz, yc, xc), out_shape=p...  46.3 us

profile of v6, /device:TPU:73, one launch (start us, length us, event | category | flops | bytes accessed | tf_op | source)
XLA Modules:
  0.0 47.0 jit_solution(18122958247057978050)
XLA Ops:
  0.0 46.3 %shard_map.82 = f32[4,24,768]{2,1,0:T(8,128)S(1)} custom-call(f32[4,24,768]{2,1,0:T(8,128)} %refs_0_.1, f32[3,8,16,64]{3,2,1,0:T(8,128)} %bitcast.1, bf16[96,40]{1,0:T(8,128)(2,1)} %constant.12.clone.refs_2_, bf16[256,768]{1,0:T(8,128)(2,1)} %constant.13.clone.refs_3_, bf16[384,128]{1,0:T(8,128)(2,1)} %constant.14.clone.refs_4_, ...), custom_call_target="tpu_custom_call" | custom-call | tf_op jit(solution)/shard_map/pallas_call | solution.py:510
  46.3 0.7 %copy.10 = f32[4,24,768]{2,1,0:T(8,128)} copy(f32[4,24,768]{2,1,0:T(8,128)S(1)} %shard_map.82) | data formatting | bytes 589824

commit v7 on v6

--- a/solution.py
+++ b/solution.py
@@ -96,9 +96,9 @@
 
 EDGE = 8
 REACH = 4
-SPAN = 24
+SPAN = 16
 TURN = 4
-WIDTHS = (1, 1, 1, 3)
+WIDTHS = (1, 1, 1, 1, 2)
 
 
 def windows(chunks):
@@ -324,9 +324,13 @@
 
     def target(step):
         some = gy // 8
+        middle = s < 3 * gy // 4
         near = jnp.where(step <= s, s - step, step)
-        late = jnp.where(step <= s, s + some - step, step)
-        late = jnp.where(step <= some, lax.rem(s + step, some), late)
+        late = s + some - step
+        late = jnp.where(middle & (late < 2 * some), late - some, late)
+        late = jnp.where(step <= s, late, step)
+        first = jnp.where(middle, some, 0) + lax.rem(s + step, some)
+        late = jnp.where(step <= some, first, late)
         return jnp.where((s >= gy // 2) & (step > 0), late, near)
 
     def build(step):

time: 47.1 us -> 46.6 us (0.989)
  the two profiles are of different devices: /device:TPU:73 before, /device:TPU:1 now
where the time goes in v7:
time: 46.6 us; the launch traced here: 46.5 us
  Pallas kernels  45.8 us (98%)
  local copies, waits for them, and re-layouts  0.72 us (2%)
    pallas_call x1, Pallas kernels, local(): pl.pallas_call(functools.partial(kernel, gz, gy, nz, yc, xc), out_shape=p...  45.8 us

profile of v7, /device:TPU:1, one launch (start us, length us, event | category | flops | bytes accessed | tf_op | source)
XLA Modules:
  0.0 46.5 jit_solution(11101814902521550932)
XLA Ops:
  0.0 45.8 %shard_map.82 = f32[4,24,768]{2,1,0:T(8,128)S(1)} custom-call(f32[4,24,768]{2,1,0:T(8,128)} %refs_0_.1, f32[3,8,16,64]{3,2,1,0:T(8,128)} %bitcast.1, bf16[96,40]{1,0:T(8,128)(2,1)} %constant.12.clone.refs_2_, bf16[256,768]{1,0:T(8,128)(2,1)} %constant.13.clone.refs_3_, bf16[384,128]{1,0:T(8,128)(2,1)} %constant.14.clone.refs_4_, ...), custom_call_target="tpu_custom_call" | custom-call | tf_op jit(solution)/shard_map/pallas_call | solution.py:514
  45.8 0.7 %copy.10 = f32[4,24,768]{2,1,0:T(8,128)} copy(f32[4,24,768]{2,1,0:T(8,128)S(1)} %shard_map.82) | data formatting | bytes 589824
